TPU v7x, 32 devices: a whole 2x2x4 slice. The times are simulated.
32 devices in a mesh: fsdp: 4 (over y, x), context: 2 (over core), tensor: 4 (over z).
Axes of the slice: x: 2, y: 2, z: 4, core: 2. Of those that a mesh axis runs over, the one named last changes fastest.
Arguments:
- tokens: bfloat16 [1024, 4, 1024], P('context', 'fsdp'), may hold values from -6 to 6
- out_grad: bfloat16 [1024, 4, 1024], P('context', 'fsdp'), may hold values from -6 to 6
- weight_stack: bfloat16 [4, 4, 1312, 1024], P('fsdp', 'tensor', 'context'), as said below
- muon_state: float32 [4, 4, 1312, 1024], P('fsdp', 'tensor', 'context'), as said below
- norm_gains: float32 [2, 1024], replicated, may hold values from 0.5 to 1.5
- adam_first: float32 [2, 1024], replicated, may hold values from -112 to 112
- adam_second: float32 [2, 1024], replicated, may hold values from 122.88 to 1228.8
- segment_ids: int32 [1024, 4], P(None, 'fsdp'), may hold values from 0 to 1024, as said below
- position_ids: int32 [1024, 4], P('context', 'fsdp'), may hold values from 0 to 1023, as said below
Outputs:
- layer_out: bfloat16 [1024, 4, 1024], P('context', 'fsdp')
- tokens_grad: bfloat16 [1024, 4, 1024], P('context', 'fsdp')
- weight_grads: float32 [4, 4, 1312, 1024], P('fsdp', 'tensor', 'context')
- muon_next: float32 [4, 4, 1312, 1024], P('fsdp', 'tensor', 'context')
- weight_update: float32 [4, 4, 1312, 1024], P('fsdp', 'tensor', 'context')
- direction_scale: float32 [4], P('fsdp')
- gain_grads: float32 [2, 1024], replicated
- adam_first_next: float32 [2, 1024], replicated
- adam_second_next: float32 [2, 1024], replicated
- gain_update: float32 [2, 1024], replicated
Inputs may be any that keep to these rules, and one draw needn't show every extreme that they name: `segment_ids`: along a sequence the nonzero ids start at 1 and rise by at most one from one token to the next; id 0 marks padding, a possibly empty run of tokens at the end of a sequence. `position_ids`: A token's offset from the first token of its document, or of the padding run. `weight_stack`: rows of a block beyond its weight's row count (R_k of the steps) are zero. `muon_state`: rows of a block beyond its weight's row count are zero.
All inputs are finite; a program needn't handle non-finite values.
Results may differ from a plain program's by a relative error of at most 0.035.
Values may be sent and summed in bfloat16 or wider, within the bound.
A program may use at most 192 MiB of HBM per device.

v0:
```python
import math

import jax
import jax.numpy as jnp
from jax import lax
from jax.sharding import PartitionSpec as P

D = 1024
HEADS = 16
HEAD_DIM = 64
FF = 2624
ITERS = 5
STEP = 8


rope_base = 160000.0
norm_eps = 1e-05
ns_first = 3.4445
ns_second = -4.775
ns_third = 2.0315
muon_beta = 0.5
muon_rate = 0.15
decay_rate = 0.1
adam_beta = 0.5
adam_rate = 0.05
ortho_eps = 1e-07
adam_eps = 1e-08
precision_highest = lax.Precision.HIGHEST


def layer_norm(values, gain_row):
    centre = values - jnp.mean(values, axis=-1, keepdims=True)
    spread = jnp.mean(centre * centre, axis=-1, keepdims=True)
    return centre * lax.rsqrt(spread + norm_eps) * gain_row


def rope_tables(positions, head_width):
    half_width = head_width // 2
    freqs = rope_base ** (-(jnp.arange(half_width, dtype=jnp.float32) * 2.0 / head_width))
    angle = positions.astype(jnp.float32)[..., None] * freqs
    angle = jnp.concatenate([angle, angle], axis=-1)
    return (jnp.cos(angle), jnp.sin(angle))


def rotate(values, cosine, sine_table):
    half_width = values.shape[-1] // 2
    turned = jnp.concatenate([-values[..., half_width:], values[..., :half_width]], axis=-1)
    return values * cosine + turned * sine_table


def rotate_back(grads_in, cosine, sine_table):
    half_width = grads_in.shape[-1] // 2
    scaled = grads_in * sine_table
    turned = jnp.concatenate([scaled[..., half_width:], -scaled[..., :half_width]], axis=-1)
    return grads_in * cosine + turned


def project(left_rows, right_rows):
    return lax.dot_general(
        left_rows, right_rows, (((1,), (1,)), ((), ())), preferred_element_type=jnp.float32
    )


def contract_exact(left_rows, right_rows):
    return lax.dot_general(
        left_rows,
        right_rows,
        (((0,), (0,)), ((), ())),
        precision=precision_highest,
        preferred_element_type=jnp.float32,
    )


def geglu_gate(gate_part, up_part):
    return jax.nn.gelu(gate_part, approximate=False) * up_part


def per_device(
    tokens,
    out_grad,
    weight_stack,
    muon_state,
    norm_gains,
    adam_first,
    adam_second,
    segment_ids,
    position_ids,
):
    local_len, seq_count, model_width = tokens.shape
    token_count = local_len * seq_count
    groups = lax.axis_size("tensor")
    contexts = lax.axis_size("context")
    full_len = local_len * contexts
    local_rows = weight_stack.shape[2]
    pad_rows = local_rows * contexts
    heads_dev = HEADS // groups
    ff_dev = FF // groups
    inner_width = heads_dev * HEAD_DIM
    counts = (3 * inner_width, inner_width, 2 * ff_dev, ff_dev)
    score_scale = HEAD_DIM ** (-0.5)
    own_block = weight_stack.reshape(local_rows, model_width)
    gathered = lax.all_gather(own_block, ("fsdp", "context"), axis=0, tiled=True).reshape(
        4, pad_rows, model_width
    )
    w_qkv = gathered[0, : counts[0]]
    w_out = gathered[1, : counts[1]]
    w_in = gathered[2, : counts[2]]
    w_down = gathered[3, : counts[3]]
    inputs = tokens.astype(jnp.float32).reshape(token_count, model_width)
    act_in = layer_norm(inputs, norm_gains[0]).astype(jnp.bfloat16)
    projected = project(act_in, w_qkv).reshape(local_len, seq_count, 3, heads_dev, HEAD_DIM)
    cosine, sine_table = rope_tables(position_ids, HEAD_DIM)
    rot_cos = cosine[:, :, None, :]
    rot_sin = sine_table[:, :, None, :]
    query_matrix = rotate(projected[:, :, 0], rot_cos, rot_sin).astype(jnp.bfloat16)
    key_matrix_rows = rotate(projected[:, :, 1], rot_cos, rot_sin).astype(jnp.bfloat16)
    value_matrix_rows = projected[:, :, 2].astype(jnp.bfloat16)
    key_value = jnp.concatenate(
        [
            key_matrix_rows.reshape(local_len, seq_count, inner_width),
            value_matrix_rows.reshape(local_len, seq_count, inner_width),
        ],
        axis=-1,
    )
    key_value_all = lax.all_gather(key_value, "context", axis=0, tiled=True)
    keys_all = key_value_all[..., :inner_width].reshape(full_len, seq_count, heads_dev, HEAD_DIM)
    values_all = key_value_all[..., inner_width:].reshape(full_len, seq_count, heads_dev, HEAD_DIM)
    offset = lax.axis_index("context") * local_len
    seg_query = lax.dynamic_slice_in_dim(segment_ids, offset, local_len, 0)
    same_doc = seg_query.T[:, :, None] == segment_ids.T[:, None, :]
    keep_mask = (seg_query > 0).astype(jnp.float32)
    unscaled_score = jnp.einsum(
        "lshd,mshd->shlm", query_matrix, keys_all, preferred_element_type=jnp.float32
    )
    scores = jnp.where(same_doc[:, None], unscaled_score * score_scale, -jnp.inf)
    row_max = jnp.max(scores, axis=-1, keepdims=True)
    log_total = row_max + jnp.log(jnp.sum(jnp.exp(scores - row_max), axis=-1, keepdims=True))
    probs_low = jnp.exp(scores - log_total).astype(jnp.bfloat16)
    attended = jnp.einsum(
        "shlm,mshd->lshd", probs_low, values_all, preferred_element_type=jnp.float32
    )
    attn_in = (
        (attended * keep_mask[:, :, None, None])
        .astype(jnp.bfloat16)
        .reshape(token_count, inner_width)
    )
    branch_one = lax.psum(
        jnp.dot(attn_in, w_out, preferred_element_type=jnp.float32).astype(jnp.bfloat16), "tensor"
    ).astype(jnp.float32)
    resid = inputs + branch_one
    mlp_in = layer_norm(resid, norm_gains[1]).astype(jnp.bfloat16)
    mixed_rows = project(mlp_in, w_in)
    hidden_full, geglu_pull = jax.vjp(geglu_gate, mixed_rows[:, :ff_dev], mixed_rows[:, ff_dev:])
    hidden = hidden_full.astype(jnp.bfloat16)
    branch_two = lax.psum(
        jnp.dot(hidden, w_down, preferred_element_type=jnp.float32).astype(jnp.bfloat16), "tensor"
    ).astype(jnp.float32)
    layer_out = (resid + branch_two).astype(jnp.bfloat16).reshape(local_len, seq_count, model_width)
    out_cot = out_grad.astype(jnp.float32).reshape(token_count, model_width)
    dbranch_two = out_cot.astype(jnp.bfloat16)
    dhidden = project(dbranch_two, w_down)
    dgate, dup_part = geglu_pull(dhidden)
    dmixed = jnp.concatenate([dgate, dup_part], axis=1).astype(jnp.bfloat16)
    dnormed_two = lax.psum(
        jnp.dot(dmixed, w_in, preferred_element_type=jnp.float32).astype(jnp.bfloat16), "tensor"
    ).astype(jnp.float32)
    norm_two_out, norm_two_pull = jax.vjp(layer_norm, resid, norm_gains[1])
    dresid_norm, dgain_two = norm_two_pull(dnormed_two)
    dresid = out_cot + dresid_norm
    dbranch_one = dresid.astype(jnp.bfloat16)
    keep_low = keep_mask.reshape(token_count, 1).astype(jnp.bfloat16)
    dattended = project(dbranch_one, w_out).astype(jnp.bfloat16) * keep_low
    dattn = dattended.reshape(local_len, seq_count, heads_dev, HEAD_DIM)
    dquery_list = []
    dkey_list = []
    dvalue_list = []
    for head_index in range(heads_dev):
        query_head = query_matrix[:, :, head_index]
        key_head = keys_all[:, :, head_index]
        value_head = values_all[:, :, head_index]
        dout_head = dattn[:, :, head_index]
        raw_head = jnp.einsum(
            "lsd,msd->slm", query_head, key_head, preferred_element_type=jnp.float32
        )
        prob_head = jnp.exp(
            jnp.where(same_doc, raw_head * score_scale, -jnp.inf) - log_total[:, head_index]
        )
        dprob = jnp.einsum(
            "lsd,msd->slm", dout_head, value_head, preferred_element_type=jnp.float32
        )
        delta = jnp.sum(prob_head * dprob, axis=-1, keepdims=True)
        dscore = (prob_head * (dprob - delta) * score_scale).astype(jnp.bfloat16)
        dquery_list.append(
            jnp.einsum("slm,msd->lsd", dscore, key_head, preferred_element_type=jnp.float32)
        )
        dkey_head = jnp.einsum(
            "slm,lsd->msd", dscore, query_head, preferred_element_type=jnp.float32
        )
        dvalue_head = jnp.einsum(
            "slm,lsd->msd",
            prob_head.astype(jnp.bfloat16),
            dout_head,
            preferred_element_type=jnp.float32,
        )
        summed = lax.psum_scatter(
            jnp.concatenate([dkey_head, dvalue_head], axis=-1).astype(jnp.bfloat16),
            "context",
            scatter_dimension=0,
            tiled=True,
        ).astype(jnp.float32)
        dkey_list.append(summed[..., :HEAD_DIM])
        dvalue_list.append(summed[..., HEAD_DIM:])
    dqueries = jnp.stack(dquery_list, axis=2)
    dkeys = jnp.stack(dkey_list, axis=2)
    dvalues = jnp.stack(dvalue_list, axis=2)
    dprojected = (
        jnp.stack(
            [
                rotate_back(dqueries, rot_cos, rot_sin),
                rotate_back(dkeys, rot_cos, rot_sin),
                dvalues,
            ],
            axis=2,
        )
        .astype(jnp.bfloat16)
        .reshape(token_count, 3 * inner_width)
    )
    dnormed_one = lax.psum(
        jnp.dot(dprojected, w_qkv, preferred_element_type=jnp.float32).astype(jnp.bfloat16),
        "tensor",
    ).astype(jnp.float32)
    norm_one_out, norm_one_pull = jax.vjp(layer_norm, inputs, norm_gains[0])
    dinput_norm, dgain_one = norm_one_pull(dnormed_one)
    tokens_grad = (
        (dresid + dinput_norm).astype(jnp.bfloat16).reshape(local_len, seq_count, model_width)
    )
    gain_grads = lax.psum(jnp.stack([dgain_one, dgain_two]), ("fsdp", "context"))

    def padded(block, used_rows):
        return jnp.pad(block, ((0, 0), (0, pad_rows - used_rows)))

    left_rows = jnp.concatenate(
        [
            padded(dprojected, counts[0]),
            padded(attn_in, counts[1]),
            padded(dmixed, counts[2]),
            padded(hidden, counts[3]),
        ],
        axis=1,
    )
    right_rows = jnp.stack([act_in, dbranch_one, mlp_in, dbranch_two])
    blocks = local_rows * lax.axis_size(("fsdp", "context")) // pad_rows
    col_block = left_rows.reshape(token_count, blocks, pad_rows)
    grad_block = lax.psum_scatter(
        jnp.einsum(
            "nbp,bnd->bpd", col_block, right_rows, preferred_element_type=jnp.float32
        ).reshape(local_rows * lax.axis_size(("fsdp", "context")), model_width),
        ("fsdp", "context"),
        scatter_dimension=0,
        tiled=True,
    )
    momentum = muon_state.reshape(local_rows, model_width)
    muon_next = muon_beta * momentum + (1.0 - muon_beta) * grad_block
    direction = (1.0 - muon_beta) * grad_block + muon_beta * muon_next
    norm_total = lax.psum(jnp.sum(direction * direction), ("context", "tensor"))
    norm_size = jnp.sqrt(norm_total)
    direction_scale = jnp.log(norm_size).reshape(1)
    ortho_local = direction / (norm_size + ortho_eps)
    ortho_block = lax.all_gather(
        ortho_local.astype(jnp.bfloat16), "context", axis=0, tiled=True
    ).astype(ortho_local.dtype)
    for sweep_index in range(ITERS):
        gram_sum = lax.psum(
            contract_exact(ortho_block, ortho_block).astype(jnp.bfloat16), "tensor"
        ).astype(jnp.float32)
        square = jnp.dot(
            gram_sum, gram_sum, precision=precision_highest, preferred_element_type=jnp.float32
        )
        mix_matrix = ns_second * gram_sum + ns_third * square
        ortho_block = ns_first * ortho_block + jnp.dot(
            ortho_block, mix_matrix, precision=precision_highest, preferred_element_type=jnp.float32
        )
    own_rows = lax.dynamic_slice_in_dim(
        ortho_block, lax.axis_index("context") * local_rows, local_rows, 0
    )
    owner_index = lax.axis_index("fsdp")
    spreads = jnp.array(
        [0.2 * math.sqrt(3 * D), 0.2 * math.sqrt(D), 0.2 * math.sqrt(2 * FF), 0.2 * math.sqrt(FF)],
        jnp.float32,
    )
    spread = jnp.sum(jnp.where(jnp.arange(4) == owner_index, spreads, 0.0))
    old_weight = own_block.astype(jnp.float32)
    weight_update = -muon_rate * (spread * own_rows + decay_rate * old_weight)
    adam_first_next = adam_beta * adam_first + (1.0 - adam_beta) * gain_grads
    adam_second_next = adam_beta * adam_second + (1.0 - adam_beta) * gain_grads * gain_grads
    correction = 1.0 - adam_beta**STEP
    gain_update = -adam_rate * (
        adam_first_next / correction / (jnp.sqrt(adam_second_next / correction) + adam_eps)
        + decay_rate * norm_gains
    )
    block_shape = (1, 1, local_rows, model_width)
    return (
        layer_out,
        tokens_grad,
        grad_block.reshape(block_shape),
        muon_next.reshape(block_shape),
        weight_update.reshape(block_shape),
        direction_scale,
        gain_grads,
        adam_first_next,
        adam_second_next,
        gain_update,
    )


def solution(mesh):
    return jax.shard_map(
        per_device,
        mesh=mesh,
        in_specs=(
            P("context", "fsdp", None),
            P("context", "fsdp", None),
            P("fsdp", "tensor", "context", None),
            P("fsdp", "tensor", "context", None),
            P(),
            P(),
            P(),
            P(None, "fsdp"),
            P("context", "fsdp"),
        ),
        out_specs=(
            P("context", "fsdp", None),
            P("context", "fsdp", None),
            P("fsdp", "tensor", "context", None),
            P("fsdp", "tensor", "context", None),
            P("fsdp", "tensor", "context", None),
            P("fsdp"),
            P(),
            P(),
            P(),
            P(),
        ),
        check_vma=False,
    )
```

profile of v0, /device:TPU:0, one launch (start us, length us, event | category | flops | bytes accessed | tf_op | source)
XLA Modules:
  0.0 1234.4 jit_solution(412026081176043939)
XLA Ops:
  10.3 66.6 %all-gather.9.cloned.1.call-done = bf16[1,1,5248,1024]{3,2,1,0:T(8,128)(2,1)} async-done(((bf16[1,1,656,1024]{3,2,1,0:T(8,128)(2,1)}), bf16[1,1,5248,1024]{3,2,1,0:T(8,128)(2,1)}) %all-gather.9.cloned.1.call-update) | async-done | bytes 10747920 | tf_op jit(solution)/shard_map/all_gather | solution.py:102
  84.7 6.6 all-gather.5.cloned.1.call-done
  94.4 2.4 exponential_reduce_fusion
  99.2 2.6 convolution_convert_fusion.6
  102.0 53.0 %all-reduce.12.cloned.1.call-done = bf16[512,1024]{1,0:T(8,128)(2,1)} async-done(((bf16[512,1024]{1,0:T(8,128)(2,1)}), bf16[512,1024]{1,0:T(8,128)(2,1)}) %all-reduce.12.cloned.1.call-update) | async-done | bytes 1048592 | tf_op jit(solution)/shard_map/psum | solution.py:147
  157.2 3.6 fusion.46
  160.8 5.0 add_convert_fusion.2
  167.5 4.8 fusion.85
  176.5 47.2 %all-reduce.14.cloned.1.call-done = bf16[512,1024]{1,0:T(8,128)(2,1)} async-done(((bf16[512,1024]{1,0:T(8,128)(2,1)}), bf16[512,1024]{1,0:T(8,128)(2,1)}) %all-reduce.14.cloned.1.call-update) | async-done | bytes 1048592 | tf_op jit(solution)/shard_map/psum | solution.py:164
  223.7 2.9 fusion.57
  240.8 2.6 multiply_reduce_fusion.3
  253.3 2.6 fusion.108
  272.2 4.3 reduce-scatter.10.cloned.1.call-done
  279.4 8.8 reduce-scatter.12.cloned.1.call-done
  295.9 10.6 fusion.1
  306.5 140.0 %reduce-scatter.14.cloned.1.call-done = f32[656,1024]{1,0:T(8,128)} async-done(((f32[5248,1024]{1,0:T(8,128)}), f32[656,1024]{1,0:T(8,128)}) %reduce-scatter.14.cloned.1.call-update) | async-done | bytes 2686992 | tf_op jit(solution)/shard_map/reduce_scatter | solution.py:254
  446.5 3.9 multiply_reduce_fusion
  450.4 16.9 %psum.81 = f32[]{:T(128)} all-reduce(f32[]{:T(128)} %multiply_reduce_fusion), channel_id=1, replica_groups=mesh['fsdp'=4,'context'=2,'tensor'=4] {'context','tensor'}, use_global_device_ids=true, to_apply=%region_25.26 | all-reduce | flops 1 | bytes 8 | tf_op jit(solution)/shard_map/psum | solution.py:265
  468.0 5.5 fusion.47
  473.6 9.3 all-gather.7.cloned.1.call-done
  482.8 7.4 convolution_convert_fusion.4
  490.4 87.2 %all-reduce.16.cloned.1.call-done = bf16[1024,1024]{1,0:T(8,128)(2,1)} async-done(((bf16[1024,1024]{1,0:T(8,128)(2,1)}), bf16[1024,1024]{1,0:T(8,128)(2,1)}) %all-reduce.16.cloned.1.call-update) | async-done | bytes 2097168 | tf_op jit(solution)/shard_map/psum | solution.py:273
  577.7 4.7 fusion.184
  582.4 9.2 multiply_add_fusion.3
  591.7 2.4 copy-done.78
  594.0 21.3 %convolution_convert_fusion.3 = bf16[1024,1024]{1,0:T(8,128)(2,1)} fusion(f32[1312,1024]{1,0:T(8,128)S(1)} %multiply_add_fusion.3), kind=kOutput, calls=%fused_computation.123 | convolution fusion | flops 16509829120 | bytes 7471104 | tf_op jit(solution)/shard_map/dot_general | solution.py:65
  615.5 85.3 %all-reduce.18.cloned.1.call-done = bf16[1024,1024]{1,0:T(8,128)(2,1)} async-done(((bf16[1024,1024]{1,0:T(8,128)(2,1)}), bf16[1024,1024]{1,0:T(8,128)(2,1)}) %all-reduce.18.cloned.1.call-update) | async-done | bytes 2097168 | tf_op jit(solution)/shard_map/psum | solution.py:273
  700.7 4.7 fusion.185
  705.4 22.6 %multiply_add_fusion.2 = f32[1312,1024]{1,0:T(8,128)S(1)} fusion(f32[1312,1024]{1,0:T(8,128)} %copy-done.78, f32[1024,1024]{1,0:T(8,128)S(1)} %fusion.185, bf16[1024,1024]{1,0:T(8,128)(2,1)S(1)} %copy-done.74), kind=kOutput, calls=%fused_computation.6 | convolution fusion | flops 16515661824 | bytes 17039360 | tf_op jit(solution)/shard_map/dot_general | solution.py:280
  728.0 2.4 copy-done.79
  730.4 21.3 %convolution_convert_fusion.2 = bf16[1024,1024]{1,0:T(8,128)(2,1)} fusion(f32[1312,1024]{1,0:T(8,128)S(1)} %multiply_add_fusion.2), kind=kOutput, calls=%fused_computation.122 | convolution fusion | flops 16509829120 | bytes 7471104 | tf_op jit(solution)/shard_map/dot_general | solution.py:65
  751.8 85.3 %all-reduce.20.cloned.1.call-done = bf16[1024,1024]{1,0:T(8,128)(2,1)} async-done(((bf16[1024,1024]{1,0:T(8,128)(2,1)}), bf16[1024,1024]{1,0:T(8,128)(2,1)}) %all-reduce.20.cloned.1.call-update) | async-done | bytes 2097168 | tf_op jit(solution)/shard_map/psum | solution.py:273
  837.1 4.7 fusion.186
  841.8 22.4 %multiply_add_fusion.1 = f32[1312,1024]{1,0:T(8,128)S(1)} fusion(f32[1312,1024]{1,0:T(8,128)} %copy-done.79, f32[1024,1024]{1,0:T(8,128)S(1)} %fusion.186, bf16[1024,1024]{1,0:T(8,128)(2,1)S(1)} %copy-done.75), kind=kOutput, calls=%fused_computation.5 | convolution fusion | flops 16515661824 | bytes 17039360 | tf_op jit(solution)/shard_map/dot_general | solution.py:280
  864.2 2.4 copy-done.77
  866.6 21.6 %convolution_convert_fusion.1 = bf16[1024,1024]{1,0:T(8,128)(2,1)} fusion(f32[1312,1024]{1,0:T(8,128)S(1)} %multiply_add_fusion.1), kind=kOutput, calls=%fused_computation.121 | convolution fusion | flops 16509829120 | bytes 7471104 | tf_op jit(solution)/shard_map/dot_general | solution.py:65
  888.4 3.4 convolution_convert_fusion.5
  891.8 3.7 fusion.82
  895.5 78.0 %all-reduce.22.cloned.1.call-done = bf16[1024,1024]{1,0:T(8,128)(2,1)} async-done(((bf16[1024,1024]{1,0:T(8,128)(2,1)}), bf16[1024,1024]{1,0:T(8,128)(2,1)}) %all-reduce.22.cloned.1.call-update) | async-done | bytes 2097168 | tf_op jit(solution)/shard_map/psum | solution.py:273
  973.5 4.7 fusion.187
  978.2 22.2 %multiply_add_fusion = f32[1312,1024]{1,0:T(8,128)S(1)} fusion(f32[1312,1024]{1,0:T(8,128)} %copy-done.77, f32[1024,1024]{1,0:T(8,128)S(1)} %fusion.187, bf16[1024,1024]{1,0:T(8,128)(2,1)S(1)} %copy-done.72), kind=kOutput, calls=%fused_computation.4 | convolution fusion | flops 16515661824 | bytes 17039360 | tf_op jit(solution)/shard_map/dot_general | solution.py:280
  1000.4 2.4 copy-done.35
  1002.8 21.5 %convolution_convert_fusion = bf16[1024,1024]{1,0:T(8,128)(2,1)} fusion(f32[1312,1024]{1,0:T(8,128)S(1)} %multiply_add_fusion), kind=kOutput, calls=%fused_computation.120 | convolution fusion | flops 16509829120 | bytes 7471104 | tf_op jit(solution)/shard_map/dot_general | solution.py:65
  1026.3 152.3 %all-reduce.24.cloned.1.call-done = (bf16[512,1024]{1,0:T(8,128)(2,1)}, bf16[512,1024]{1,0:T(8,128)(2,1)}, bf16[1024,1024]{1,0:T(8,128)(2,1)}) async-done(((bf16[512,1024]{1,0:T(8,128)(2,1)}, bf16[512,1024]{1,0:T(8,128)(2,1)}, bf16[1024,1024]{1,0:T(8,128)(2,1)}), (bf16[512,1024]{1,0:T(8,128)(2,1)}, bf16[512,1024]{1,0:T(8,128)(2,1)}, bf16[1024,1024]{1,0:T(8,128)(2,1)})) %all-reduce.24.cloned.1.call-update) | async-done | bytes 4194320 | tf_op jit(solution)/shard_map/psum | solution.py:155
  1181.7 13.7 %psum.87 = f32[2,1024]{1,0:T(2,128)S(1)} all-reduce(f32[2,1024]{1,0:T(2,128)S(1)} %pad_maximum_fusion.11), channel_id=1, replica_groups=mesh['fsdp'=4,'context'=2,'tensor'=4] {'fsdp','context'}, use_global_device_ids=true, to_apply=%region_33.34 | all-reduce | flops 2048 | bytes 16384 | tf_op jit(solution)/shard_map/psum | solution.py:237
  1195.4 4.7 fusion.188
  1200.2 20.2 %fusion.9 = f32[1312,1024]{1,0:T(8,128)S(1)} fusion(f32[1312,1024]{1,0:T(8,128)} %copy-done.35, f32[1024,1024]{1,0:T(8,128)S(1)} %fusion.188, bf16[1024,1024]{1,0:T(8,128)(2,1)S(1)} %copy-done.71), kind=kOutput, calls=%fused_computation.16 | convolution fusion | flops 16512974848 | bytes 17039360 | tf_op jit(solution)/shard_map/dot_general | solution.py:280
  1221.2 3.0 fusion.35
  (290 shorter events, 82.9 us)
Async XLA Ops:
  7.2 3.1 copy-start.57
  7.2 69.7 %all-gather.9.cloned.1.call-start = ((), (), s32[]{:S(2)}) async-start(), calls=%async_computation.18 | async-start | bytes 12091392 | tf_op jit(solution)/shard_map/all_gather | solution.py:102
  7.9 83.4 %all-gather.5.cloned.1.call-start = ((), (), s32[]{:S(2)}) async-start(), calls=%async_computation.5 | async-start | bytes 1572864 | tf_op jit(solution)/shard_map/all_gather | solution.py:125
  10.2 162.4 %copy-start.60 = (f32[512]{0:T(512)}, f32[512]{0:T(512)S(1)}, u32[]{:S(2)}) copy-start(f32[512]{0:T(512)S(1)} %fusion.155) | copy-start | bytes 6148
  79.6 13.1 %copy-start.25 = (f32[512,1,3,4,64]{0,4,3,2,1:T(8,128)}, f32[512,1,3,4,64]{0,4,3,2,1:T(8,128)S(1)}, u32[]{:S(2)}) copy-start(f32[512,1,3,4,64]{0,4,3,2,1:T(8,128)S(1)} %convolution_bitcast_fusion) | copy-start | bytes 4718596
  82.1 72.9 %all-reduce.12.cloned.1.call-start = ((), (), s32[]{:S(2)}) async-start(), calls=%async_computation.6 | async-start | bytes 2097152 | tf_op jit(solution)/shard_map/psum | solution.py:147
  92.7 4.2 copy-start.31
  101.8 121.9 %all-reduce.14.cloned.1.call-start = ((), (), s32[]{:S(2)}) async-start(), calls=%async_computation.7 | async-start | bytes 2097152 | tf_op jit(solution)/shard_map/psum | solution.py:164
  157.2 3.6 copy-start.22
  167.5 4.8 copy-start.27
  172.4 96.6 %reduce-scatter.6.cloned.1.call-start = ((), (), s32[]{:S(2)}) async-start(), calls=%async_computation.8 | async-start | bytes 393216 | tf_op jit(solution)/shard_map/reduce_scatter | solution.py:205
  231.8 6.3 copy-start.38
  240.7 29.9 %reduce-scatter.8.cloned.1.call-start = ((), (), s32[]{:S(2)}) async-start(), calls=%async_computation.9 | async-start | bytes 393216 | tf_op jit(solution)/shard_map/reduce_scatter | solution.py:205
  252.5 3.3 copy-start.7
  257.7 3.6 copy-start.14
  257.7 7.4 copy-start.12
  257.7 18.7 %reduce-scatter.10.cloned.1.call-start = ((), (), s32[]{:S(2)}) async-start(), calls=%async_computation.10 | async-start | bytes 393216 | tf_op jit(solution)/shard_map/reduce_scatter | solution.py:205
  263.3 3.9 copy-start.16
  263.3 24.8 %reduce-scatter.12.cloned.1.call-start = ((), (), s32[]{:S(2)}) async-start(), calls=%async_computation.11 | async-start | bytes 393216 | tf_op jit(solution)/shard_map/reduce_scatter | solution.py:205
  268.5 20.6 %copy-start.33 = (f32[64,512]{1,0:T(8,128)S(1)}, f32[64,512]{1,0:T(8,128)}, u32[]{:S(2)}) copy-start(f32[64,512]{1,0:T(8,128)} %fusion.151) | copy-start | bytes 393220
  268.5 20.6 %copy-start.34 = (f32[64,512]{1,0:T(8,128)S(1)}, f32[64,512]{1,0:T(8,128)}, u32[]{:S(2)}) copy-start(f32[64,512]{1,0:T(8,128)} %fusion.152) | copy-start | bytes 393220
  268.5 178.0 %reduce-scatter.14.cloned.1.call-start = ((), (), s32[]{:S(2)}) async-start(), calls=%async_computation.12 | async-start | bytes 24182784 | tf_op jit(solution)/shard_map/reduce_scatter | solution.py:254
  306.4 176.4 %all-gather.7.cloned.1.call-start = ((), (), s32[]{:S(2)}) async-start(), calls=%async_computation.13 | async-start | bytes 4030464 | tf_op jit(solution)/shard_map/all_gather | solution.py:269
  473.5 104.2 %all-reduce.16.cloned.1.call-start = ((), (), s32[]{:S(2)}) async-start(), calls=%async_computation.14 | async-start | bytes 4194304 | tf_op jit(solution)/shard_map/psum | solution.py:273
  490.2 210.5 %all-reduce.18.cloned.1.call-start = ((), (), s32[]{:S(2)}) async-start(), calls=%async_computation.15 | async-start | bytes 4194304 | tf_op jit(solution)/shard_map/psum | solution.py:273
  577.7 4.7 copy-start.70
  577.7 4.7 copy-start.73
  615.4 221.7 %all-reduce.20.cloned.1.call-start = ((), (), s32[]{:S(2)}) async-start(), calls=%async_computation.16 | async-start | bytes 4194304 | tf_op jit(solution)/shard_map/psum | solution.py:273
  700.7 4.7 copy-start.74
  751.8 221.7 %all-reduce.22.cloned.1.call-start = ((), (), s32[]{:S(2)}) async-start(), calls=%async_computation.17 | async-start | bytes 4194304 | tf_op jit(solution)/shard_map/psum | solution.py:273
  837.1 4.7 copy-start.75
  888.1 290.4 %all-reduce.24.cloned.1.call-start = ((), (), s32[]{:S(2)}) async-start(), calls=%async_computation.19 | async-start | bytes 8388608 | tf_op jit(solution)/shard_map/psum | solution.py:155
  888.4 3.4 copy-start.48
  973.5 4.7 copy-start.72
  1024.4 156.0 %copy-start.63 = (f32[512]{0:T(512)S(1)}, f32[512]{0:T(512)}, u32[]{:S(2)}) copy-start(f32[512]{0:T(512)} %copy-done.62) | copy-start | bytes 6148
  1024.4 156.0 %copy-start.61 = (f32[512]{0:T(512)S(1)}, f32[512]{0:T(512)}, u32[]{:S(2)}) copy-start(f32[512]{0:T(512)} %copy-done.60) | copy-start | bytes 6148
  1178.6 3.1 copy-start.66
  1195.4 25.0 %copy-start.59 = (f32[2,1024]{1,0:T(2,128)}, f32[2,1024]{1,0:T(2,128)S(1)}, u32[]{:S(2)}) copy-start(f32[2,1024]{1,0:T(2,128)S(1)} %psum.87) | copy-start | bytes 24580
  1195.4 4.7 copy-start.71
  1195.4 25.7 %slice-start = ((s8[5373952]{0:T(1024)(128)(4,1)}), s8[4194304]{0:T(1024)(128)(4,1)S(1)}, s32[]{:S(2)}) async-start(s8[5373952]{0:T(1024)(128)(4,1)} %bitcast.440), calls=%async_computation.20 | async-start | bytes 8388608
  1200.1 20.3 %copy-start.58 = (f32[2,1024]{1,0:T(2,128)S(1)}, f32[2,1024]{1,0:T(2,128)}, u32[]{:S(2)}) copy-start(f32[2,1024]{1,0:T(2,128)} %param.14) | copy-start | bytes 24580
  1200.2 20.3 %copy-start.68 = (f32[2,1024]{1,0:T(2,128)S(1)}, f32[2,1024]{1,0:T(2,128)}, u32[]{:S(2)}) copy-start(f32[2,1024]{1,0:T(2,128)} %param.16) | copy-start | bytes 24580
  1200.2 20.3 %copy-start.69 = (f32[2,1024]{1,0:T(2,128)S(1)}, f32[2,1024]{1,0:T(2,128)}, u32[]{:S(2)}) copy-start(f32[2,1024]{1,0:T(2,128)} %param.15) | copy-start | bytes 24580
  1200.2 20.9 %copy-start.20 = (bf16[1,1,656,1024]{3,2,1,0:T(8,128)(2,1)S(1)}, bf16[1,1,656,1024]{3,2,1,0:T(8,128)(2,1)}, u32[]{:S(2)}) copy-start(bf16[1,1,656,1024]{3,2,1,0:T(8,128)(2,1)} %param.12) | copy-start | bytes 4030468
  1200.2 20.9 %slice-start.1 = ((s8[5373952]{0:T(1024)(128)(4,1)}), s8[1179648]{0:T(1024)(128)(4,1)S(1)}, s32[]{:S(2)}) async-start(s8[5373952]{0:T(1024)(128)(4,1)} %bitcast.440), calls=%async_computation.21 | async-start | bytes 2359296
  1221.1 3.1 copy-start.2
  1221.1 3.0 copy-start.9
  1221.1 3.0 copy-start.47
  (49 other events, 78.8 us)
Sparse Core Ops, SparseCore 0:
  9.9 66.9 all-gather.8
  82.3 9.0 all-gather.4
  101.9 53.0 all-reduce.11
  172.5 51.1 all-reduce.13
  240.9 7.0 reduce-scatter.5
  257.8 6.9 reduce-scatter.7
  267.6 8.7 reduce-scatter.9
  279.2 8.8 reduce-scatter.11
  306.6 139.8 reduce-scatter.13
  473.6 9.1 all-gather.6
  490.3 87.2 all-reduce.15
  615.5 85.1 all-reduce.17
  751.9 85.1 all-reduce.19
  888.3 85.1 all-reduce.21
  1024.5 154.0 all-reduce.23
where the time goes:
time: 1240 us; the launch traced here: 1230 us
  waiting for transfers between devices  825 us (67%)
  matrix products  280 us (23%)
  other arithmetic  51 us (4%)
  blocking collectives  30.6 us (2%)
  local copies, waits for them, and re-layouts  29.1 us (2%)
  between operations  17.8 us (1%)
    psum x4, waiting for transfers between devices, per_device(): lax.psum(contract_exact(ortho_block, ortho_block).astype(jnp.bfloat16), '...  336 us
    psum x1, waiting for transfers between devices, per_device(): lax.psum(jnp.dot(hidden, w_down, preferred_element_type=jnp.float32).asty...  152 us
    reduce_scatter x1, waiting for transfers between devices, per_device(): lax.psum_scatter(jnp.einsum('nbp,bnd->bpd', col_block, right_rows, prefer...  140 us
    dot_general x5, matrix products, per_device(): jnp.dot(ortho_block, mix_matrix, precision=precision_highest, preferred_e...  96.6 us
    dot_general x5, matrix products, contract_exact(): lax.dot_general(left_rows, right_rows, (((0,), (0,)), ((), ())), precisio...  93.1 us
    all_gather x1, waiting for transfers between devices, per_device(): lax.all_gather(own_block, ('fsdp', 'context'), axis=0, tiled=True)  66.6 us
    psum x1, waiting for transfers between devices, per_device(): lax.psum(jnp.dot(attn_in, w_out, preferred_element_type=jnp.float32).asty...  53 us
    psum x1, waiting for transfers between devices, per_device(): lax.psum(jnp.dot(dmixed, w_in, preferred_element_type=jnp.float32).astype...  47.2 us
  transfers between devices with their start and end apart: 15, of which 13 were waited for; matrix products, arithmetic and copies ran while one was open for 4% of the time, Pallas kernels for 0%

commit v1 on v0

--- a/solution.py
+++ b/solution.py
@@ -3,6 +3,8 @@
 import jax
 import jax.numpy as jnp
 from jax import lax
+from jax.experimental import pallas as pl
+from jax.experimental.pallas import tpu as pltpu
 from jax.sharding import PartitionSpec as P
 
 D = 1024
@@ -313,9 +315,744 @@
     )
 
 
+MESH_ID = pl.DeviceIdType.MESH
+ANY = pl.ANY
+
+
+def ring_place(index):
+    return index + index // 2 - 2 * (index // 3)
+
+
+def split_units(rows, parts, unit=16):
+    units = rows // unit
+    sizes = [(units // parts + (1 if i < units % parts else 0)) * unit for i in range(parts)]
+    return [s for s in sizes if s]
+
+
+def ring_chunks(counts, local_rows, which, core, target):
+    first = core * local_rows
+    rows = min(counts[which], first + local_rows) - first
+    if rows <= 0:
+        return [[], []]
+    halves = split_units(rows, 2)
+    if len(halves) == 1:
+        halves = halves + [0]
+    out, at = [], first
+    for half in halves:
+        pieces = []
+        if half:
+            for size in split_units(half, max(1, round(half / target))):
+                pieces.append((at, size))
+                at += size
+        out.append(pieces)
+    return out
+
+
+class Place:
+    def __init__(self):
+        self.f = lax.axis_index("fsdp")
+        self.c = lax.axis_index("context")
+        self.t = lax.axis_index("tensor")
+        self.pos = ring_place(self.f)
+        self.next = ring_place((self.pos + 1) % 4)
+        self.prev = ring_place((self.pos + 3) % 4)
+        self.outer = jnp.logical_or(self.t == 0, self.t == 3)
+        self.inner_mate = jnp.where(self.t == 0, 1, 2)
+        self.outer_mate = jnp.where(self.t == 1, 0, 3)
+
+    def ring(self, direction):
+        return (self.next if direction == 0 else self.prev, self.c, self.t)
+
+    def partner(self):
+        return (self.f, 1 - self.c, self.t)
+
+    def chip_z(self, z):
+        return (self.f, self.c, z)
+
+    def hop(self, which, direction):
+        home = (0, 1, 3, 2)[which]
+        if direction == 0:
+            return (self.pos + 4 - home) % 4
+        return (home + 4 - self.pos) % 4
+
+
+def greet(place, ring, partner, line):
+    barrier = pltpu.get_barrier_semaphore()
+
+    def signal(device):
+        pl.semaphore_signal(barrier, inc=1, device_id=device, device_id_type=MESH_ID)
+
+    count = 0
+    if ring:
+        signal(place.ring(0))
+        signal(place.ring(1))
+        count += 2
+    if partner:
+        signal(place.partner())
+        count += 1
+    if line:
+        @pl.when(place.outer)
+        def _():
+            signal(place.chip_z(place.inner_mate))
+            pl.semaphore_wait(barrier, count + 1)
+
+        @pl.when(jnp.logical_not(place.outer))
+        def _():
+            signal(place.chip_z(place.outer_mate))
+            signal(place.chip_z(3 - place.t))
+            pl.semaphore_wait(barrier, count + 2)
+    else:
+        pl.semaphore_wait(barrier, count)
+
+
+def remote(src, dst, send, recv, device):
+    return pltpu.make_async_remote_copy(
+        src_ref=src, dst_ref=dst, send_sem=send, recv_sem=recv, device_id=device, device_id_type=MESH_ID
+    )
+
+
+def run_steps(*tracks):
+    total = max(len(track) for track in tracks)
+    done = [0] * len(tracks)
+    for index in range(total):
+        for number, track in enumerate(tracks):
+            upto = -(-len(track) * (index + 1) // total)
+            while done[number] < upto:
+                track[done[number]]()
+                done[number] += 1
+
+
+def gather_plan(counts, local_rows, ks, target=96):
+    plan = []
+    for core in (0, 1):
+        ident = 0
+        for which in ks:
+            for direction, pieces in enumerate(ring_chunks(counts, local_rows, which, core, target)):
+                for order, (row, rows) in enumerate(pieces):
+                    plan.append((ident, which, core, direction, order, row, rows))
+                    ident += 1
+    return plan, max(p[0] for p in plan) + 1
+
+
+def gather_steps(place, plan, local_rows, base, own_ref, out_ref, sems):
+    ss, rs, sp, rp = sems
+
+    def dst(which, row, rows):
+        return out_ref.at[pl.ds(base[which] + row, rows)]
+
+    def src(core, row, rows):
+        return own_ref.at[pl.ds(row - core * local_rows, rows)]
+
+    def begin():
+        for ident, which, core, direction, order, row, rows in plan:
+            @pl.when(jnp.logical_and(place.c == core, place.f == which))
+            def _():
+                remote(src(core, row, rows), dst(which, row, rows), ss.at[ident], rs.at[ident],
+                       place.ring(direction)).start()
+        for ident, which, core, direction, order, row, rows in plan:
+            @pl.when(jnp.logical_and(place.c == core, place.f == which))
+            def _():
+                remote(src(core, row, rows), dst(which, row, rows), sp.at[ident], rp.at[ident],
+                       place.partner()).start()
+
+    def step(item):
+        ident, which, core, direction, order, row, rows = item
+
+        def run():
+            hop = place.hop(which, direction)
+            mine = dst(which, row, rows)
+
+            @pl.when(jnp.logical_and(place.c == core, hop >= 1))
+            def _():
+                remote(mine, mine, ss.at[ident], rs.at[ident], place.ring(direction)).wait_recv()
+
+                @pl.when(hop <= 2)
+                def _():
+                    remote(mine, mine, ss.at[ident], rs.at[ident], place.ring(direction)).start()
+
+                remote(mine, mine, sp.at[ident], rp.at[ident], place.partner()).start()
+        return run
+
+    def end():
+        for ident, which, core, direction, order, row, rows in plan:
+            hop = place.hop(which, direction)
+            mine = dst(which, row, rows)
+
+            @pl.when(jnp.logical_and(place.c == core, hop <= 2))
+            def _():
+                remote(mine, mine, ss.at[ident], rs.at[ident], place.ring(direction)).wait_send()
+
+            @pl.when(place.c == core)
+            def _():
+                remote(mine, mine, sp.at[ident], rp.at[ident], place.partner()).wait_send()
+
+            @pl.when(place.c == 1 - core)
+            def _():
+                remote(mine, mine, sp.at[ident], rp.at[ident], place.partner()).wait_recv()
+
+    ordered = sorted(plan, key=lambda p: (p[4], p[1]))
+    return begin, [step(item) for item in ordered], end
+
+
+def line_steps(place, chunks, own, out, early, mid, low, sems, lag=1, back_lag=3, prep=None, done=None):
+    s1, r1, s2, r2, s3, r3 = sems
+
+    def from_end(i, device):
+        return remote(own(i), early(i), s1.at[i], r1.at[i], device)
+
+    def across(i):
+        return remote(mid(i), low(i), s2.at[i], r2.at[i], place.chip_z(3 - place.t))
+
+    def back(i, device):
+        return remote(out(i), out(i), s3.at[i], r3.at[i], device)
+
+    def step(i):
+        def run():
+            if i < chunks and prep is not None:
+                prep(i)
+
+            @pl.when(place.outer)
+            def _():
+                if i < chunks:
+                    from_end(i, place.chip_z(place.inner_mate)).start()
+                if 0 <= i - lag - back_lag < chunks:
+                    back(i - lag - back_lag, place.chip_z(place.inner_mate)).wait_recv()
+
+            @pl.when(jnp.logical_not(place.outer))
+            def _():
+                if i < chunks:
+                    from_end(i, place.chip_z(place.outer_mate)).wait_recv()
+                    pair = own(i)[...].astype(jnp.float32) + early(i)[...].astype(jnp.float32)
+                    mid(i)[...] = pair.astype(mid(i).dtype)
+                    across(i).start()
+                j = i - lag
+                if 0 <= j < chunks:
+                    across(j).wait_recv()
+                    total = mid(j)[...].astype(jnp.float32) + low(j)[...].astype(jnp.float32)
+                    out(j)[...] = total.astype(out(j).dtype)
+                    back(j, place.chip_z(place.outer_mate)).start()
+            if done is not None:
+                if 0 <= i - lag - back_lag < chunks:
+                    done(i - lag - back_lag)
+        return run
+
+    def end():
+        @pl.when(place.outer)
+        def _():
+            for i in range(chunks):
+                from_end(i, place.chip_z(place.inner_mate)).wait_send()
+
+        @pl.when(jnp.logical_not(place.outer))
+        def _():
+            for i in range(chunks):
+                across(i).wait_send()
+                back(i, place.chip_z(place.outer_mate)).wait_send()
+
+    return [step(i) for i in range(chunks + lag + back_lag)], end
+
+
+def scatter_steps(place, plan, local_rows, base, part_ref, grad_ref, prx, rrx, tx, sems):
+    ss, rs, sp, rp = sems
+
+    def rows_of(ref, which, row, rows):
+        return ref.at[pl.ds(base[which] + row, rows)]
+
+    def partner_copy(item):
+        ident, which, core, direction, order, row, rows = item
+        return remote(rows_of(part_ref, which, row, rows), rows_of(prx, which, row, rows),
+                      sp.at[ident], rp.at[ident], place.partner())
+
+    def ring_copy(item):
+        ident, which, core, direction, order, row, rows = item
+        return remote(rows_of(tx, which, row, rows), rows_of(rrx, which, row, rows),
+                      ss.at[ident], rs.at[ident], place.ring(direction))
+
+    ordered = sorted(plan, key=lambda p: (p[4], p[1]))
+    last = max(p[4] for p in plan)
+
+    def begin():
+        for item in ordered:
+            @pl.when(place.c == 1 - item[2])
+            def _():
+                partner_copy(item).start()
+
+    def visit(item, late):
+        ident, which, core, direction, order, row, rows = item
+        hop = place.hop(which, direction)
+        role = (late + 1) % 4
+
+        @pl.when(jnp.logical_and(place.c == core, hop == role))
+        def _():
+            partner_copy(item).wait_recv()
+            total = (rows_of(part_ref, which, row, rows)[...].astype(jnp.float32)
+                     + rows_of(prx, which, row, rows)[...].astype(jnp.float32))
+            if role != 1:
+                ring_copy(item).wait_recv()
+                total = total + rows_of(rrx, which, row, rows)[...].astype(jnp.float32)
+            if role == 0:
+                grad_ref[pl.ds(row - core * local_rows, rows)] = total
+            else:
+                rows_of(tx, which, row, rows)[...] = total.astype(tx.dtype)
+                ring_copy(item).start()
+
+    def step(j):
+        def run():
+            for late in range(4):
+                for item in ordered:
+                    if item[4] == j - late:
+                        visit(item, late)
+        return run
+
+    def end():
+        for item in plan:
+            ident, which, core, direction, order, row, rows = item
+
+            @pl.when(place.c == 1 - core)
+            def _():
+                partner_copy(item).wait_send()
+
+            @pl.when(jnp.logical_and(place.c == core, place.hop(which, direction) != 0))
+            def _():
+                ring_copy(item).wait_send()
+
+    return begin, [step(j) for j in range(last + 4)], end
+
+
+VMEM_SPEC = pl.BlockSpec(memory_space=pltpu.VMEM)
+ANY_SPEC = pl.BlockSpec(memory_space=pl.ANY)
+
+
+def dma(count):
+    return pltpu.SemaphoreType.DMA((count,))
+
+
+def comm_call(kernel, outs, ins, in_specs, out_specs, scratch, ident):
+    return pl.pallas_call(
+        kernel,
+        out_shape=outs,
+        in_specs=in_specs,
+        out_specs=out_specs,
+        scratch_shapes=scratch,
+        compiler_params=pltpu.CompilerParams(
+            collective_id=ident, has_side_effects=True, vmem_limit_bytes=60 * 2**20
+        ),
+    )(*ins)
+
+
+def base_rows(counts, ks):
+    base, at = {}, 0
+    for which in ks:
+        base[which] = at
+        at += counts[which]
+    return base, at
+
+
+def own_rows_copy(place, counts, local_rows, ks, base, own_ref, out_ref, sem, act):
+    for which in ks:
+        for core in (0, 1):
+            rows = min(counts[which] - core * local_rows, local_rows)
+            if rows > 0:
+                @pl.when(jnp.logical_and(place.c == core, place.f == which))
+                def _():
+                    act(pltpu.make_async_copy(
+                        own_ref.at[pl.ds(0, rows)],
+                        out_ref.at[pl.ds(base[which] + core * local_rows, rows)],
+                        sem.at[0],
+                    ))
+
+
+def gather_weights(own_block, counts, ks, ident):
+    local_rows, width = own_block.shape
+    plan, count = gather_plan(counts, local_rows, ks)
+    base, total = base_rows(counts, ks)
+
+    def kernel(own_ref, out_ref, ss, rs, sp, rp, local_sem):
+        place = Place()
+        greet(place, True, True, False)
+        begin, steps, end = gather_steps(place, plan, local_rows, base, own_ref, out_ref, (ss, rs, sp, rp))
+        begin()
+        own_rows_copy(place, counts, local_rows, ks, base, own_ref, out_ref, local_sem, lambda d: d.start())
+        run_steps(steps)
+        own_rows_copy(place, counts, local_rows, ks, base, own_ref, out_ref, local_sem, lambda d: d.wait())
+        end()
+
+    return comm_call(kernel, jax.ShapeDtypeStruct((total, width), own_block.dtype), (own_block,),
+                     [VMEM_SPEC], VMEM_SPEC, [dma(count)] * 4 + [dma(1)], ident), base
+
+
+def line_sum_and_gather(term, own_block, counts, ks, ident, chunks=8):
+    local_rows, width = own_block.shape
+    plan, count = gather_plan(counts, local_rows, ks)
+    base, total = base_rows(counts, ks)
+    rows = term.shape[0] // chunks
+
+    def kernel(term_ref, own_ref, sum_ref, out_ref, early, mid, low, *sems):
+        place = Place()
+        greet(place, True, True, True)
+        cut = lambda ref: lambda i: ref.at[pl.ds(i * rows, rows)]
+        line, line_end = line_steps(place, chunks, cut(term_ref), cut(sum_ref), cut(early), cut(mid), cut(low), sems[:6])
+        begin, steps, end = gather_steps(place, plan, local_rows, base, own_ref, out_ref, sems[6:10])
+        begin()
+        own_rows_copy(place, counts, local_rows, ks, base, own_ref, out_ref, sems[10], lambda d: d.start())
+        run_steps(line, steps)
+        own_rows_copy(place, counts, local_rows, ks, base, own_ref, out_ref, sems[10], lambda d: d.wait())
+        line_end()
+        end()
+
+    return comm_call(
+        kernel,
+        (jax.ShapeDtypeStruct(term.shape, term.dtype), jax.ShapeDtypeStruct((total, width), own_block.dtype)),
+        (term, own_block), [VMEM_SPEC] * 2, (VMEM_SPEC, VMEM_SPEC),
+        [pltpu.VMEM(term.shape, term.dtype)] * 3 + [dma(chunks)] * 6 + [dma(count)] * 4 + [dma(1)], ident,
+    ), base
+
+
+def scatter_grads(part, counts, ks, local_rows, ident, term=None, chunks=8):
+    plan, count = gather_plan(counts, local_rows, ks)
+    base, total = base_rows(counts, ks)
+    width = part.shape[1]
+    lined = term is not None
+    rows = term.shape[0] // chunks if lined else 0
+
+    def kernel(*refs):
+        part_ref, refs = refs[0], refs[1:]
+        if lined:
+            term_ref, grad_ref, sum_ref, prx, rrx, tx, early, mid, low = refs[:9]
+            sems = refs[9:]
+        else:
+            grad_ref, prx, rrx, tx = refs[:4]
+            sems = refs[4:]
+        place = Place()
+        greet(place, True, True, lined)
+        begin, steps, end = scatter_steps(place, plan, local_rows, base, part_ref, grad_ref, prx, rrx, tx, sems[:4])
+        begin()
+        grad_ref[...] = jnp.zeros_like(grad_ref)
+        if lined:
+            cut = lambda ref: lambda i: ref.at[pl.ds(i * rows, rows)]
+            line, line_end = line_steps(place, chunks, cut(term_ref), cut(sum_ref), cut(early), cut(mid), cut(low), sems[4:10])
+            run_steps(line, steps)
+            line_end()
+        else:
+            run_steps(steps)
+        end()
+
+    ins = (part, term) if lined else (part,)
+    outs = [jax.ShapeDtypeStruct((local_rows, width), jnp.float32)]
+    scratch = [pltpu.VMEM(part.shape, part.dtype)] * 3
+    sems = [dma(count)] * 4
+    if lined:
+        outs.append(jax.ShapeDtypeStruct(term.shape, term.dtype))
+        scratch += [pltpu.VMEM(term.shape, term.dtype)] * 3
+        sems += [dma(chunks)] * 6
+    return comm_call(kernel, tuple(outs), ins, [VMEM_SPEC] * len(ins), tuple([VMEM_SPEC] * len(outs)), scratch + sems, ident)
+
+
+def swap_cores(block, ident):
+    def kernel(x_ref, o_ref, send, recv):
+        place = Place()
+        greet(place, False, True, False)
+        copy = remote(x_ref, o_ref, send.at[0], recv.at[0], place.partner())
+        copy.start()
+        copy.wait()
+
+    return comm_call(kernel, jax.ShapeDtypeStruct(block.shape, block.dtype), (block,), [VMEM_SPEC], VMEM_SPEC,
+                     [dma(1), dma(1)], ident)
+
+
+def plane_sum(block, ident):
+    def kernel(x_ref, o_ref, held, send, recv):
+        f, c, t = lax.axis_index("fsdp"), lax.axis_index("context"), lax.axis_index("tensor")
+        me = f * 2 + c
+        barrier = pltpu.get_barrier_semaphore()
+
+        def device(shift):
+            other = (me + shift) % 8
+            return (other // 2, other % 2, t)
+
+        for shift in range(1, 8):
+            pl.semaphore_signal(barrier, inc=1, device_id=device(shift), device_id_type=MESH_ID)
+        pl.semaphore_wait(barrier, 7)
+        held[pl.ds(me, 1)] = x_ref[...][None]
+        copies = []
+        for shift in range(1, 8):
+            copy = remote(x_ref, held.at[me], send.at[shift], recv.at[shift], device(shift))
+            copy.start()
+            copies.append(copy)
+        for copy in copies:
+            copy.wait()
+        total = held[0]
+        for k in range(1, 8):
+            total = total + held[k]
+        o_ref[...] = total
+
+    return comm_call(kernel, jax.ShapeDtypeStruct(block.shape, block.dtype), (block,), [VMEM_SPEC], VMEM_SPEC,
+                     [pltpu.VMEM((8,) + block.shape, block.dtype), dma(8), dma(8)], ident)
+
+
+def gram_sum(rows_low, square, ident):
+    rows, width = rows_low.shape
+    tile = width // 4
+    half = tile // 2
+    chunks = 10
+
+    def kernel(x_ref, q_ref, g_ref, norm_ref, mine, theirs, prx, tot, other, early, mid, low, *sems):
+        place = Place()
+        c = place.c
+        sp, rp, st, rt = sems[6:10]
+
+        def blocks(core):
+            return [(3 * core, 3 * core), (2 * core, 2 * core + 1), (core + 1, core + 1), (core, core + 2), (core, 3 - core)]
+
+        greet(place, False, True, True)
+
+        def at(k):
+            return pl.ds(pl.multiple_of(k * tile, tile), tile)
+
+        def gram(i, j):
+            return lax.dot_general(x_ref[:, at(i)], x_ref[:, at(j)], (((0,), (0,)), ((), ())),
+                                   preferred_element_type=jnp.float32)
+
+        def partner(n):
+            sl = pl.ds(n * tile, tile)
+            return remote(theirs.at[sl], prx.at[sl], sp.at[n], rp.at[n], place.partner())
+
+        def norm_row(ref):
+            return ref.at[pl.ds(5 * tile, 8)]
+
+        for n, (i, j) in enumerate(blocks(1 - c)):
+            theirs[pl.ds(n * tile, tile)] = gram(i, j)
+            partner(n).start()
+        norm_row(theirs)[...] = jnp.broadcast_to(q_ref[0:1, 0:1], (8, tile))
+        pn = remote(norm_row(theirs), norm_row(prx), sp.at[5], rp.at[5], place.partner())
+        pn.start()
+
+        def span(i):
+            return pl.ds(i * half, half) if i < chunks - 1 else pl.ds(i * half, half + 8)
+
+        def cut(ref):
+            return lambda i: ref.at[span(i)]
+
+        def prep(i):
+            if i % 2 == 0:
+                n = i // 2
+                sl = pl.ds(n * tile, tile)
+                block = gram(*blocks(c)[n])
+                partner(n).wait_recv()
+                mine[sl] = block + prx[sl]
+            if i == chunks - 1:
+                pn.wait_recv()
+                norm_row(mine)[...] = norm_row(prx)[...] + jnp.broadcast_to(q_ref[0:1, 0:1], (8, tile))
+
+        def share(i):
+            return remote(cut(tot)(i), cut(other)(i), st.at[i], rt.at[i], place.partner())
+
+        def place_block(ref, n, core):
+            i, j = blocks(core)[n]
+            block = ref[pl.ds(n * tile, tile)]
+            g_ref[at(i), at(j)] = block
+            g_ref[at(j), at(i)] = block.T
+
+        def done(i):
+            share(i).start()
+            if i % 2 == 1:
+                place_block(tot, i // 2, c)
+            if i >= 2:
+                share(i - 2).wait_recv()
+                if (i - 2) % 2 == 1:
+                    place_block(other, (i - 2) // 2, 1 - c)
+
+        steps, end = line_steps(place, chunks, cut(mine), cut(tot), cut(early), cut(mid), cut(low), sems[:6],
+                                prep=prep, done=done)
+        run_steps(steps)
+        for i in (chunks - 2, chunks - 1):
+            share(i).wait_recv()
+        place_block(other, 4, 1 - c)
+        norm_ref[...] = jnp.broadcast_to(tot[5 * tile:5 * tile + 8, 0:128], (8, 128))
+        end()
+        for n in range(5):
+            partner(n).wait_send()
+        pn.wait_send()
+        for i in range(chunks):
+            share(i).wait_send()
+
+    packed = pltpu.VMEM((5 * tile + 8, tile), jnp.float32)
+    return comm_call(
+        kernel,
+        (jax.ShapeDtypeStruct((width, width), jnp.float32), jax.ShapeDtypeStruct((8, 128), jnp.float32)),
+        (rows_low, square), [VMEM_SPEC] * 2, (VMEM_SPEC, VMEM_SPEC),
+        [packed] * 8 + [dma(chunks)] * 6 + [dma(6), dma(6), dma(chunks), dma(chunks)], ident,
+    )
+
+
+def per_device_block(tokens, out_grad, weight_stack, muon_state, norm_gains, adam_first, adam_second, segment_ids,
+                     position_ids):
+    token_count, _, model_width = tokens.shape
+    groups, contexts = 4, 2
+    full_len = token_count * contexts
+    local_rows = weight_stack.shape[2]
+    heads_dev = HEADS // groups
+    ff_dev = FF // groups
+    inner_width = heads_dev * HEAD_DIM
+    counts = (3 * inner_width, inner_width, 2 * ff_dev, ff_dev)
+    score_scale = HEAD_DIM ** (-0.5)
+    own_block = weight_stack.reshape(local_rows, model_width)
+    low = jnp.bfloat16
+    context = lax.axis_index("context")
+
+    first_weights, base = gather_weights(own_block, counts, (0, 1), 0)
+    w_qkv = first_weights[: counts[0]]
+    w_out = first_weights[counts[0]:]
+    inputs = tokens.astype(jnp.float32).reshape(token_count, model_width)
+    act_in = layer_norm(inputs, norm_gains[0]).astype(low)
+    projected = project(act_in, w_qkv).reshape(token_count, 3, heads_dev, HEAD_DIM)
+    cosine, sine_table = rope_tables(position_ids.reshape(token_count), HEAD_DIM)
+    rot_cos = cosine[:, None, :]
+    rot_sin = sine_table[:, None, :]
+    queries = rotate(projected[:, 0], rot_cos, rot_sin).astype(low)
+    keys = rotate(projected[:, 1], rot_cos, rot_sin).astype(low)
+    values = projected[:, 2].astype(low)
+    mine = jnp.concatenate([keys.reshape(token_count, inner_width), values.reshape(token_count, inner_width)], axis=1)
+    theirs = swap_cores(mine, 1)
+    key_value = jnp.concatenate([mine, theirs], axis=0)
+    keys_all = key_value[:, :inner_width].reshape(full_len, heads_dev, HEAD_DIM)
+    values_all = key_value[:, inner_width:].reshape(full_len, heads_dev, HEAD_DIM)
+    segments = segment_ids.reshape(full_len)
+    seg_query = lax.dynamic_slice_in_dim(segments, context * token_count, token_count, 0)
+    seg_other = lax.dynamic_slice_in_dim(segments, (1 - context) * token_count, token_count, 0)
+    seg_key = jnp.concatenate([seg_query, seg_other])
+    same_doc = (seg_query[:, None] == seg_key[None, :])[None]
+    keep_mask = (seg_query > 0).astype(jnp.float32)[:, None]
+    raw = jnp.einsum("lhd,mhd->hlm", queries, keys_all, preferred_element_type=jnp.float32)
+    scores = jnp.where(same_doc, raw * score_scale, -jnp.inf)
+    row_max = jnp.max(scores, axis=-1, keepdims=True)
+    log_total = row_max + jnp.log(jnp.sum(jnp.exp(scores - row_max), axis=-1, keepdims=True))
+    probs = jnp.exp(scores - log_total)
+    probs_low = probs.astype(low)
+    attended = jnp.einsum("hlm,mhd->lhd", probs_low, values_all, preferred_element_type=jnp.float32)
+    attn_in = (attended.reshape(token_count, inner_width) * keep_mask).astype(low)
+    branch_term = jnp.dot(attn_in, w_out, preferred_element_type=jnp.float32).astype(low)
+    (branch_one, last_weights), _ = line_sum_and_gather(branch_term, own_block, counts, (2, 3), 2)
+    w_in = last_weights[: counts[2]]
+    w_down = last_weights[counts[2]:]
+    resid = inputs + branch_one.astype(jnp.float32)
+    mlp_in = layer_norm(resid, norm_gains[1]).astype(low)
+    mixed_rows = project(mlp_in, w_in)
+    hidden_full, geglu_pull = jax.vjp(geglu_gate, mixed_rows[:, :ff_dev], mixed_rows[:, ff_dev:])
+    hidden = hidden_full.astype(low)
+    branch_two_term = jnp.dot(hidden, w_down, preferred_element_type=jnp.float32).astype(low)
+    out_low = out_grad.reshape(token_count, model_width)
+    out_cot = out_low.astype(jnp.float32)
+    dgate, dup_part = geglu_pull(project(out_low, w_down))
+    dmixed = jnp.concatenate([dgate, dup_part], axis=1).astype(low)
+    dnormed_two_term = jnp.dot(dmixed, w_in, preferred_element_type=jnp.float32).astype(low)
+
+    def grad_term(left, right):
+        return lax.dot_general(left, right, (((0,), (0,)), ((), ())), preferred_element_type=jnp.float32).astype(low)
+
+    late_terms = jnp.concatenate([grad_term(dmixed, mlp_in), grad_term(hidden, out_low)], axis=0)
+    grad_late, dnormed_two = scatter_grads(late_terms, counts, (2, 3), local_rows, 3, dnormed_two_term)
+    _, norm_two_pull = jax.vjp(layer_norm, resid, norm_gains[1])
+    dresid_norm, dgain_two = norm_two_pull(dnormed_two.astype(jnp.float32))
+    dresid = out_cot + dresid_norm
+    dbranch_one = dresid.astype(low)
+    dattended = project(dbranch_one, w_out).astype(low) * keep_mask.astype(low)
+    dattn = dattended.reshape(token_count, heads_dev, HEAD_DIM)
+    dprobs = jnp.einsum("lhd,mhd->hlm", dattn, values_all, preferred_element_type=jnp.float32)
+    delta = jnp.sum(probs * dprobs, axis=-1, keepdims=True)
+    dscores = (probs * (dprobs - delta) * score_scale).astype(low)
+    dqueries = jnp.einsum("hlm,mhd->lhd", dscores, keys_all, preferred_element_type=jnp.float32)
+    dkeys = jnp.einsum("hlm,lhd->mhd", dscores, queries, preferred_element_type=jnp.float32)
+    dvalues = jnp.einsum("hlm,lhd->mhd", probs_low, dattn, preferred_element_type=jnp.float32)
+    dkv = jnp.concatenate([dkeys.reshape(full_len, inner_width), dvalues.reshape(full_len, inner_width)], axis=1)
+    dkv_other = swap_cores(dkv[token_count:].astype(low), 4)
+    dkv_own = dkv[:token_count] + dkv_other.astype(jnp.float32)
+    dkeys = dkv_own[:, :inner_width].reshape(token_count, heads_dev, HEAD_DIM)
+    dprojected = jnp.concatenate(
+        [
+            rotate_back(dqueries, rot_cos, rot_sin).reshape(token_count, inner_width),
+            rotate_back(dkeys, rot_cos, rot_sin).reshape(token_count, inner_width),
+            dkv_own[:, inner_width:],
+        ],
+        axis=1,
+    ).astype(low)
+    early_terms = jnp.concatenate([grad_term(dprojected, act_in), grad_term(attn_in, dbranch_one)], axis=0)
+    (grad_early,) = scatter_grads(early_terms, counts, (0, 1), local_rows, 5)
+    dnormed_one_term = jnp.dot(dprojected, w_qkv, preferred_element_type=jnp.float32).astype(low)
+
+    owner_index = lax.axis_index("fsdp")
+    grad_block = jnp.where(owner_index >= 2, grad_late, grad_early)
+    momentum = muon_state.reshape(local_rows, model_width)
+    muon_next = muon_beta * momentum + (1.0 - muon_beta) * grad_block
+    direction = (1.0 - muon_beta) * grad_block + muon_beta * muon_next
+    direction_low = direction.astype(low)
+    square = jnp.sum(direction * direction).reshape(1, 1)
+    gram, norm_total = gram_sum(direction_low, jnp.broadcast_to(square, (8, 128)), 6)
+    norm_size = jnp.sqrt(norm_total[0, 0])
+    direction_scale = jnp.log(norm_size).reshape(1)
+    inverse = 1.0 / (norm_size + ortho_eps)
+    branch_two_term, dnormed_one_term, gram = lax.optimization_barrier((branch_two_term, dnormed_one_term, gram))
+    branch_two = lax.psum(branch_two_term, "tensor").astype(jnp.float32)
+    dnormed_one = lax.psum(dnormed_one_term, "tensor").astype(jnp.float32)
+
+    power = gram * (inverse * inverse)
+    ortho = direction_low.astype(jnp.float32) * inverse
+    high = lax.Precision.HIGH
+
+    def times(left, right):
+        return jnp.dot(left, right, precision=high, preferred_element_type=jnp.float32)
+
+    for sweep_index in range(ITERS):
+        square_power = times(power, power)
+        mix = ns_second * power + ns_third * square_power
+        ortho = ns_first * ortho + jnp.dot(ortho.astype(low), mix.astype(low), preferred_element_type=jnp.float32)
+        if sweep_index < ITERS - 1:
+            cube = times(power, square_power)
+            tail = (2.0 * ns_second * ns_third) * square_power + (ns_third * ns_third) * cube
+            power = (
+                (ns_first * ns_first) * power
+                + (2.0 * ns_first * ns_second) * square_power
+                + (ns_second * ns_second + 2.0 * ns_first * ns_third) * cube
+                + times(square_power, tail)
+            )
+
+    layer_out = (resid + branch_two).astype(low).reshape(tokens.shape)
+    _, norm_one_pull = jax.vjp(layer_norm, inputs, norm_gains[0])
+    dinput_norm, dgain_one = norm_one_pull(dnormed_one)
+    tokens_grad = (dresid + dinput_norm).astype(low).reshape(tokens.shape)
+    gain_grads = plane_sum(jnp.concatenate([jnp.stack([dgain_one, dgain_two])] * 4, axis=0), 7)[:2]
+    spreads = jnp.array(
+        [0.2 * math.sqrt(3 * D), 0.2 * math.sqrt(D), 0.2 * math.sqrt(2 * FF), 0.2 * math.sqrt(FF)],
+        jnp.float32,
+    )
+    spread = jnp.sum(jnp.where(jnp.arange(4) == owner_index, spreads, 0.0))
+    weight_update = -muon_rate * (spread * ortho + decay_rate * own_block.astype(jnp.float32))
+    adam_first_next = adam_beta * adam_first + (1.0 - adam_beta) * gain_grads
+    adam_second_next = adam_beta * adam_second + (1.0 - adam_beta) * gain_grads * gain_grads
+    correction = 1.0 - adam_beta**STEP
+    gain_update = -adam_rate * (
+        adam_first_next / correction / (jnp.sqrt(adam_second_next / correction) + adam_eps)
+        + decay_rate * norm_gains
+    )
+    block_shape = (1, 1, local_rows, model_width)
+    return (
+        layer_out,
+        tokens_grad,
+        grad_block.reshape(block_shape),
+        muon_next.reshape(block_shape),
+        weight_update.reshape(block_shape),
+        direction_scale,
+        gain_grads,
+        adam_first_next,
+        adam_second_next,
+        gain_update,
+    )
+
+
 def solution(mesh):
+    sizes = dict(mesh.shape)
+    block = (sizes["fsdp"], sizes["context"], sizes["tensor"]) == (4, 2, 4)
     return jax.shard_map(
-        per_device,
+        per_device_block if block else per_device,
         mesh=mesh,
         in_specs=(
             P("context", "fsdp", None),

time: 1240 us -> 682 us (0.55)
  waiting for transfers between devices: 825 us -> 0.02 us
  Pallas kernels: 0 us -> 366 us
  matrix products: 280 us -> 221 us
  blocking collectives: 30.6 us -> 0 us
    psum x7 -> x1, waiting for transfers between devices: 588 us -> 0.01 us  [per_device_block(): branch_two = lax.psum(branch_two_term, 'tensor').astype(jnp.float32)]
    pallas_call x0 -> x8, Pallas kernels: none -> 366 us  [comm_call(): pl.pallas_call(kernel, out_shape=outs, in_specs=in_specs, out_specs=out_s...]
    reduce_scatter x5 -> x0, waiting for transfers between devices: 153 us -> none  [the longest x1 140 us: per_device(): lax.psum_scatter(jnp.einsum('nbp,bnd->bpd', col_block, right_rows, prefer...]
    all_gather x3 -> x0, waiting for transfers between devices: 82.5 us -> none  [the longest x1 66.6 us: per_device(): lax.all_gather(own_block, ('fsdp', 'context'), axis=0, tiled=True)]
    dot_general x42 -> x32, matrix products: 268 us -> 212 us  [the longest x13 117 us: times(): jnp.dot(left, right, precision=high, preferred_element_type=jnp.float32)]
    psum x2 -> x0, blocking collectives: 30.6 us -> none  [the longest x1 16.9 us: per_device(): norm_total = lax.psum(jnp.sum(direction * direction), ('context', 'tensor'))]
    unnamed x168 -> x96, local copies, waits for them, and re-layouts: 20.9 us -> 3.84 us
  transfers between devices with their start and end apart: 15 -> 1, of which waited for: 13 -> 0; matrix products, arithmetic and copies ran while one was open for 4% -> 21% of each run, Pallas kernels for 0% -> 0%
where the time goes in v1:
time: 682 us; the launch traced here: 679 us
  Pallas kernels  366 us (54%)
  matrix products  221 us (32%)
  other arithmetic  51.3 us (8%)
  local copies, waits for them, and re-layouts  22.2 us (3%)
  between operations  17.8 us (3%)
    pallas_call x8, Pallas kernels, comm_call(): pl.pallas_call(kernel, out_shape=outs, in_specs=in_specs, out_specs=out_s...  366 us
    dot_general x13, matrix products, times(): jnp.dot(left, right, precision=high, preferred_element_type=jnp.float32)  117 us
    dot_general x1, matrix products, per_device_block(): jnp.einsum('hlm,lhd->mhd', dscores, queries, preferred_element_type=jnp.f...  23.8 us
    dot_general x1, matrix products, per_device_block(): jnp.einsum('hlm,mhd->lhd', dscores, keys_all, preferred_element_type=jnp....  22.8 us
    dot_general x5, matrix products, per_device_block(): jnp.dot(ortho.astype(low), mix.astype(low), preferred_element_type=jnp.fl...  20.7 us
  transfers between devices with their start and end apart: 1, of which 0 were waited for; matrix products, arithmetic and copies ran while one was open for 21% of the time, Pallas kernels for 0%

profile of v1, /device:TPU:0, one launch (start us, length us, event | category | flops | bytes accessed | tf_op | source)
XLA Modules:
  0.0 678.6 jit_solution(615155740095906465)
XLA Ops:
  11.2 40.0 %shard_map.177 = bf16[1024,1024]{1,0:T(8,128)(2,1)} custom-call(bf16[656,1024]{1,0:T(8,128)(2,1)} %bitcast.175), custom_call_target="tpu_custom_call" | custom-call | tf_op jit(solution)/shard_map/pallas_call | solution.py:630
  60.4 2.1 fusion.149
  62.5 2.0 copy.35
  67.7 3.8 shard_map.178
  74.8 2.4 exponential_reduce_fusion
  78.0 2.3 fusion.196
  81.9 163.4 %shard_map.179 = (bf16[512,1024]{1,0:T(8,128)(2,1)}, bf16[1968,1024]{1,0:T(8,128)(2,1)}) custom-call(bf16[512,1024]{1,0:T(8,128)(2,1)} %convolution_convert_fusion.5.term_ref, bf16[656,1024]{1,0:T(8,128)(2,1)} %bitcast.176), custom_call_target="tpu_custom_call" | custom-call | tf_op jit(solution)/shard_map/pallas_call | solution.py:630
  247.5 3.7 fusion.61
  251.2 3.8 add_convert_fusion.19
  255.7 2.0 convolution_convert_fusion.4
  258.5 2.8 fusion.107.refs_1_
  263.1 2.3 pad_maximum_fusion.refs_0_
  265.4 65.5 %shard_map.180 = (f32[656,1024]{1,0:T(8,128)}, bf16[512,1024]{1,0:T(8,128)(2,1)}) custom-call(bf16[1968,1024]{1,0:T(8,128)(2,1)} %pad_maximum_fusion.refs_0_, bf16[512,1024]{1,0:T(8,128)(2,1)} %fusion.107.refs_1_), custom_call_target="tpu_custom_call" | custom-call | tf_op jit(solution)/shard_map/pallas_call | solution.py:630
  331.0 2.4 fusion.66
  338.0 3.2 fusion.194
  341.2 4.5 fusion.208
  347.3 23.8 %fusion.7 = f32[4,64,1024]{2,1,0:T(8,128)} fusion(bf16[512,4,64]{0,2,1:T(8,128)(2,1)S(1)} %get-tuple-element.67, f32[4,512,1024]{2,1,0:T(8,128)} %fusion.208, f32[4,512,1024]{2,1,0:T(8,128)} %copy-done.1, f32[4,512]{1,0:T(4,128)} %copy-done.30, pred[512,1024]{1,0:T(8,128)(4,1)} %copy-done.14), kind=kOutput, calls=%fused_computation.9 | convolution fusion | flops 291507200 | bytes 18620416 | tf_op jit(solution)/shard_map/hlm,lhd->mhd/dot_general | solution.py:964
  371.1 2.5 copy.39
  375.5 3.8 shard_map.181
  382.1 22.8 %broadcast_multiply_fusion.1 = (f32[512,4,64]{0,2,1:T(8,128)S(1)}, f32[512,4,64]{0,2,1:T(8,128)}, f32[512,4,64]{0,2,1:T(8,128)}) fusion(f32[512,64]{0,1:T(8,128)S(1)} %copy-done.21, f32[512,4,64]{0,2,1:T(8,128)S(1)} %bitcast.189, bf16[1024,4,64]{0,2,1:T(8,128)(2,1)} %bitcast.178, f32[4,512,1024]{2,1,0:T(8,128)} %fusion.208, f32[4,512,1024]{2,1,0:T(8,128)} %copy-done.1, ...), kind=kOutput, calls=%fused_computation.213 | convolution fusion | flops 291769344 | bytes 20062208 | tf_op jit(solution)/shard_map/hlm,mhd->lhd/dot_general | solution.py:963
  408.9 2.0 copy.43
  412.3 3.6 convolution_convert_fusion.3
  415.9 2.3 convolution_convert_fusion.1
  418.2 2.9 pad_maximum_fusion.1.refs_0_
  421.1 35.5 %shard_map.182 = f32[656,1024]{1,0:T(8,128)} custom-call(bf16[1024,1024]{1,0:T(8,128)(2,1)} %pad_maximum_fusion.1.refs_0_), custom_call_target="tpu_custom_call" | custom-call | tf_op jit(solution)/shard_map/pallas_call | solution.py:630
  456.6 5.5 fusion.63
  462.1 2.5 multiply_reduce_fusion.1
  465.9 47.2 %shard_map.183 = (f32[1024,1024]{1,0:T(8,128)}, f32[8,128]{1,0:T(8,128)}) custom-call(bf16[656,1024]{1,0:T(8,128)(2,1)} %get-tuple-element.47.x_ref, f32[8,128]{1,0:T(8,128)} %broadcast_in_dim.29.q_ref), custom_call_target="tpu_custom_call" | custom-call | tf_op jit(solution)/shard_map/pallas_call | solution.py:630
  515.1 11.2 %fusion.46 = f32[1024,1024]{1,0:T(8,128)S(1)} fusion(f32[1024,1024]{1,0:T(8,128)} %get-tuple-element.27, f32[]{:T(128)S(6)} %mul.544), kind=kOutput, calls=%fused_computation.48 | convolution fusion | flops 6443499520 | bytes 8388612 | tf_op jit(solution)/shard_map/dot_general | solution.py:1002
  526.3 3.2 multiply_add_fusion.3
  529.6 7.0 %fusion.44 = f32[1024,1024]{1,0:T(8,128)S(1)} fusion(f32[1024,1024]{1,0:T(8,128)S(1)} %fusion.46, f32[1024,1024]{1,0:T(8,128)S(1)} %copy-done.37, f32[]{:T(128)S(6)} %mul.544), kind=kOutput, calls=%fused_computation.46 | convolution fusion | flops 6443499520 | bytes 12582916 | tf_op jit(solution)/shard_map/dot_general | solution.py:1002
  536.6 8.1 %add_add_fusion.3 = f32[1024,1024]{1,0:T(8,128)S(1)} fusion(f32[1024,1024]{1,0:T(8,128)S(1)} %fusion.44, f32[1024,1024]{1,0:T(8,128)S(1)} %fusion.46, f32[1024,1024]{1,0:T(8,128)S(1)} %copy-done.37, f32[]{:T(128)S(6)} %mul.544), kind=kOutput, calls=%fused_computation.34 | convolution fusion | flops 6452936704 | bytes 16777220 | tf_op jit(solution)/shard_map/dot_general | solution.py:1002
  544.7 7.0 %fusion.209 = f32[1024,1024]{1,0:T(8,128)S(1)} fusion(f32[1024,1024]{1,0:T(8,128)S(1)} %add_add_fusion.3), kind=kOutput, calls=%fused_computation.280 | convolution fusion | flops 6442450944 | bytes 8388608 | tf_op jit(solution)/shard_map/dot_general | solution.py:1002
  551.7 7.2 %fusion.210 = f32[1024,1024]{1,0:T(8,128)S(1)} fusion(f32[1024,1024]{1,0:T(8,128)S(1)} %add_add_fusion.3, f32[1024,1024]{1,0:T(8,128)S(1)} %fusion.209), kind=kOutput, calls=%fused_computation.281 | convolution fusion | flops 6442450944 | bytes 12582912 | tf_op jit(solution)/shard_map/dot_general | solution.py:1002
  559.0 3.3 multiply_add_fusion.2
  562.2 7.7 %add_add_fusion.2 = f32[1024,1024]{1,0:T(8,128)S(1)} fusion(f32[1024,1024]{1,0:T(8,128)S(1)} %fusion.210, f32[1024,1024]{1,0:T(8,128)S(1)} %fusion.209, f32[1024,1024]{1,0:T(8,128)S(1)} %add_add_fusion.3), kind=kOutput, calls=%fused_computation.28 | convolution fusion | flops 6451888128 | bytes 16777216 | tf_op jit(solution)/shard_map/dot_general | solution.py:1002
  570.0 7.2 %fusion.211 = f32[1024,1024]{1,0:T(8,128)S(1)} fusion(f32[1024,1024]{1,0:T(8,128)S(1)} %add_add_fusion.2), kind=kOutput, calls=%fused_computation.282 | convolution fusion | flops 6442450944 | bytes 8388608 | tf_op jit(solution)/shard_map/dot_general | solution.py:1002
  577.2 7.1 %fusion.212 = f32[1024,1024]{1,0:T(8,128)S(1)} fusion(f32[1024,1024]{1,0:T(8,128)S(1)} %add_add_fusion.2, f32[1024,1024]{1,0:T(8,128)S(1)} %fusion.211), kind=kOutput, calls=%fused_computation.283 | convolution fusion | flops 6442450944 | bytes 12582912 | tf_op jit(solution)/shard_map/dot_general | solution.py:1002
  584.3 3.7 multiply_add_fusion.1
  588.0 7.7 %add_add_fusion.1 = f32[1024,1024]{1,0:T(8,128)S(1)} fusion(f32[1024,1024]{1,0:T(8,128)S(1)} %fusion.212, f32[1024,1024]{1,0:T(8,128)S(1)} %fusion.211, f32[1024,1024]{1,0:T(8,128)S(1)} %add_add_fusion.2), kind=kOutput, calls=%fused_computation.22 | convolution fusion | flops 6451888128 | bytes 16777216 | tf_op jit(solution)/shard_map/dot_general | solution.py:1002
  595.8 7.2 %fusion.213 = f32[1024,1024]{1,0:T(8,128)S(1)} fusion(f32[1024,1024]{1,0:T(8,128)S(1)} %add_add_fusion.1), kind=kOutput, calls=%fused_computation.284 | convolution fusion | flops 6442450944 | bytes 8388608 | tf_op jit(solution)/shard_map/dot_general | solution.py:1002
  603.0 7.1 %fusion.214 = f32[1024,1024]{1,0:T(8,128)S(1)} fusion(f32[1024,1024]{1,0:T(8,128)S(1)} %add_add_fusion.1, f32[1024,1024]{1,0:T(8,128)S(1)} %fusion.213), kind=kOutput, calls=%fused_computation.285 | convolution fusion | flops 6442450944 | bytes 12582912 | tf_op jit(solution)/shard_map/dot_general | solution.py:1002
  610.1 8.6 %fusion.12 = f32[1024,1024]{1,0:T(8,128)} fusion(f32[1024,1024]{1,0:T(8,128)S(1)} %fusion.213, f32[1024,1024]{1,0:T(8,128)S(1)} %fusion.214), kind=kOutput, calls=%fused_computation.12 | convolution fusion | flops 6445596672 | bytes 12582912 | tf_op jit(solution)/shard_map/dot_general | solution.py:1002
  618.8 3.3 multiply_add_fusion
  623.3 23.7 %add_convert_fusion = bf16[1024,1024]{1,0:T(8,128)(2,1)} fusion(f32[1024,1024]{1,0:T(8,128)} %fusion.12, f32[1024,1024]{1,0:T(8,128)} %copy-done.42, f32[1024,1024]{1,0:T(8,128)} %copy-done.41, f32[1024,1024]{1,0:T(8,128)} %copy-done.40), kind=kOutput, calls=%fused_computation.11 | convolution fusion | flops 6459228160 | bytes 18874368 | tf_op jit(solution)/shard_map/dot_general | solution.py:1002
  647.1 7.2 %multiply_bitcast_fusion = f32[1,1,656,1024]{3,2,1,0:T(8,128)} fusion(f32[656,1024]{1,0:T(8,128)} %multiply_add_fusion, bf16[1024,1024]{1,0:T(8,128)(2,1)} %add_convert_fusion, f32[]{:T(128)} %fusion.160, bf16[1,1,656,1024]{3,2,1,0:T(8,128)(2,1)S(1)} %copy-done.9), kind=kOutput, calls=%fused_computation.56 | convolution fusion | flops 1381105664 | bytes 8814596 | tf_op jit(solution)/shard_map/dot_general | solution.py:1007
  658.0 7.1 %shard_map.184 = f32[8,1024]{1,0:T(8,128)} custom-call(f32[8,1024]{1,0:T(8,128)} %concatenate.69.x_ref), custom_call_target="tpu_custom_call" | custom-call | tf_op jit(solution)/shard_map/pallas_call | solution.py:630
  665.2 3.8 fusion.147
  (168 shorter events, 51.5 us)
Async XLA Ops:
  7.2 647.1 %all-reduce.3.cloned.1.call-start = ((), (), s32[]{:S(2)}) async-start(), calls=%async_computation | async-start | bytes 4194304 | tf_op jit(solution)/shard_map/psum | solution.py:994
  10.3 40.8 %copy-start.27 = (f32[512]{0:T(512)}, f32[512]{0:T(512)S(1)}, u32[]{:S(2)}) copy-start(f32[512]{0:T(512)S(1)} %fusion.158) | copy-start | bytes 6148
  11.2 40.0 %copy-start = (bf16[512,1,1024]{2,0,1:T(8,128)(2,1)S(1)}, bf16[512,1,1024]{2,0,1:T(8,128)(2,1)}, u32[]{:S(2)}) copy-start(bf16[512,1,1024]{2,0,1:T(8,128)(2,1)} %param.10) | copy-start | bytes 3145732
  51.2 1.4 slice-start.2
  53.7 1.1 copy-start.18
  53.7 2.3 copy-start.35
  53.8 2.3 copy-start.34
  58.6 279.3 %copy-start.14 = (pred[512,1024]{1,0:T(8,128)(4,1)}, pred[512,1024]{1,0:T(8,128)(4,1)S(1)}, u32[]{:S(2)}) copy-start(pred[512,1024]{1,0:T(8,128)(4,1)S(1)} %broadcast_compare_fusion) | copy-start | bytes 1572868
  58.9 6.7 copy-start.13
  72.9 1.9 copy-start.19
  74.7 3.3 copy-start.1
  77.2 3.2 copy-start.30
  78.0 2.3 copy-start.29
  78.0 2.4 copy-start.7
  245.3 1.7 copy-start.2
  247.5 3.7 copy-start.16
  247.5 3.7 copy-start.38
  330.9 2.5 copy-start.15
  331.0 7.0 %slice-start = ((s8[8388608]{0:T(1024)(128)(4,1)}), s8[4194304]{0:T(1024)(128)(4,1)S(1)}, s32[]{:S(2)}) async-start(s8[8388608]{0:T(1024)(128)(4,1)} %bitcast.171), calls=%async_computation.1 | async-start | bytes 8388608
  333.4 1.2 copy-start.17
  333.4 4.5 slice-start.1
  334.4 1.9 copy-start.3
  334.6 2.8 copy-start.8
  334.6 2.8 copy-start.36
  334.9 3.0 copy-start.31
  379.4 2.7 copy-start.21
  404.9 6.1 copy-start.12
  412.3 3.6 copy-start.22
  412.3 3.6 copy-start.23
  412.3 3.6 copy-start.28
  415.9 2.3 copy-start.20
  456.6 5.5 copy-start.4
  462.1 2.5 copy-start.5
  515.0 11.3 %copy-start.10 = (bf16[656,1024]{1,0:T(8,128)(2,1)S(1)}, bf16[656,1024]{1,0:T(8,128)(2,1)}, u32[]{:S(2)}) copy-start(bf16[656,1024]{1,0:T(8,128)(2,1)} %get-tuple-element.47.x_ref) | copy-start | bytes 4030468
  515.1 11.3 %copy-start.37 = (f32[1024,1024]{1,0:T(8,128)S(1)}, f32[1024,1024]{1,0:T(8,128)}, u32[]{:S(2)}) copy-start(f32[1024,1024]{1,0:T(8,128)} %get-tuple-element.27) | copy-start | bytes 12582916
  551.7 7.3 %copy-start.43 = (f32[656,1024]{1,0:T(8,128)S(1)}, f32[656,1024]{1,0:T(8,128)}, u32[]{:S(2)}) copy-start(f32[656,1024]{1,0:T(8,128)} %multiply_add_fusion.3) | copy-start | bytes 8060932
  577.2 7.1 %copy-start.45 = (f32[656,1024]{1,0:T(8,128)S(1)}, f32[656,1024]{1,0:T(8,128)}, u32[]{:S(2)}) copy-start(f32[656,1024]{1,0:T(8,128)} %multiply_add_fusion.2) | copy-start | bytes 8060932
  595.8 22.9 %copy-start.40 = (f32[1024,1024]{1,0:T(8,128)}, f32[1024,1024]{1,0:T(8,128)S(1)}, u32[]{:S(2)}) copy-start(f32[1024,1024]{1,0:T(8,128)S(1)} %add_add_fusion.1) | copy-start | bytes 12582916
  603.0 15.7 %copy-start.41 = (f32[1024,1024]{1,0:T(8,128)}, f32[1024,1024]{1,0:T(8,128)S(1)}, u32[]{:S(2)}) copy-start(f32[1024,1024]{1,0:T(8,128)S(1)} %fusion.213) | copy-start | bytes 12582916
  610.1 8.6 %copy-start.42 = (f32[1024,1024]{1,0:T(8,128)}, f32[1024,1024]{1,0:T(8,128)S(1)}, u32[]{:S(2)}) copy-start(f32[1024,1024]{1,0:T(8,128)S(1)} %fusion.214) | copy-start | bytes 12582916
  610.1 8.6 %copy-start.44 = (f32[656,1024]{1,0:T(8,128)S(1)}, f32[656,1024]{1,0:T(8,128)}, u32[]{:S(2)}) copy-start(f32[656,1024]{1,0:T(8,128)} %multiply_add_fusion.1) | copy-start | bytes 8060932
  618.7 4.0 copy-start.39
  623.3 23.7 %copy-start.9 = (bf16[1,1,656,1024]{3,2,1,0:T(8,128)(2,1)S(1)}, bf16[1,1,656,1024]{3,2,1,0:T(8,128)(2,1)}, u32[]{:S(2)}) copy-start(bf16[1,1,656,1024]{3,2,1,0:T(8,128)(2,1)} %param.12) | copy-start | bytes 4030468
  647.1 9.1 %copy-start.26 = (f32[512]{0:T(512)S(1)}, f32[512]{0:T(512)}, u32[]{:S(2)}) copy-start(f32[512]{0:T(512)} %copy-done.25) | copy-start | bytes 6148
  654.2 1.9 copy-start.6
  665.1 3.9 copy-start.24
  665.2 3.9 copy-start.32
  665.2 3.9 copy-start.33
  (2 other events, 1.9 us)
Sparse Core Ops, SparseCore 0:
  513.2 84.2 all-reduce.2

commit v2 on v1

--- a/solution.py
+++ b/solution.py
@@ -455,22 +455,26 @@
                 remote(src(core, row, rows), dst(which, row, rows), sp.at[ident], rp.at[ident],
                        place.partner()).start()
 
-    def step(item):
+    ordered = sorted(plan, key=lambda p: (p[4], p[1]))
+    last = max(p[4] for p in plan)
+
+    def visit(item, role):
         ident, which, core, direction, order, row, rows = item
-
+        mine = dst(which, row, rows)
+
+        @pl.when(jnp.logical_and(place.c == core, place.hop(which, direction) == role))
+        def _():
+            remote(mine, mine, ss.at[ident], rs.at[ident], place.ring(direction)).wait_recv()
+            if role <= 2:
+                remote(mine, mine, ss.at[ident], rs.at[ident], place.ring(direction)).start()
+            remote(mine, mine, sp.at[ident], rp.at[ident], place.partner()).start()
+
+    def step(j):
         def run():
-            hop = place.hop(which, direction)
-            mine = dst(which, row, rows)
-
-            @pl.when(jnp.logical_and(place.c == core, hop >= 1))
-            def _():
-                remote(mine, mine, ss.at[ident], rs.at[ident], place.ring(direction)).wait_recv()
-
-                @pl.when(hop <= 2)
-                def _():
-                    remote(mine, mine, ss.at[ident], rs.at[ident], place.ring(direction)).start()
-
-                remote(mine, mine, sp.at[ident], rp.at[ident], place.partner()).start()
+            for role in (1, 2, 3):
+                for item in ordered:
+                    if item[4] == j - (role - 1):
+                        visit(item, role)
         return run
 
     def end():
@@ -490,8 +494,7 @@
             def _():
                 remote(mine, mine, sp.at[ident], rp.at[ident], place.partner()).wait_recv()
 
-    ordered = sorted(plan, key=lambda p: (p[4], p[1]))
-    return begin, [step(item) for item in ordered], end
+    return begin, [step(j) for j in range(last + 3)], end
 
 
 def line_steps(place, chunks, own, out, early, mid, low, sems, lag=1, back_lag=3, prep=None, done=None):
@@ -882,6 +885,215 @@
         (rows_low, square), [VMEM_SPEC] * 2, (VMEM_SPEC, VMEM_SPEC),
         [packed] * 8 + [dma(chunks)] * 6 + [dma(6), dma(6), dma(chunks), dma(chunks)], ident,
     )
+
+
+def halves(value):
+    high = value.astype(jnp.bfloat16)
+    return high, (value - high.astype(jnp.float32)).astype(jnp.bfloat16)
+
+
+def gaps(fixed, moved):
+    return [(fixed * (index + 1)) // moved for index in range(moved)]
+
+
+def iterate(gram, norm, direction_low, own_block, branch_term, resid, dgains, norm_gains, adam_first, adam_second, ident):
+    rows, width = direction_low.shape
+    tile = 256
+    parts = width // tile
+    tokens = branch_term.shape[0]
+    chunks = 8
+    step_rows = tokens // chunks
+    aa = ns_first * ns_first
+    ab = 2.0 * ns_first * ns_second
+    bbac = ns_second * ns_second + 2.0 * ns_first * ns_third
+    bc = 2.0 * ns_second * ns_third
+    cc = ns_third * ns_third
+    correction = 1.0 - adam_beta**STEP
+
+    def kernel(g_ref, n_ref, d_ref, w_ref, t_ref, r_ref, dg_ref, gain_ref, af_ref, as_ref,
+               u_ref, lo_ref, gg_ref, afn_ref, asn_ref, gu_ref,
+               p_ref, ph, pl_, hh, hl, uh, ul, mx, x_ref, early, mid, low, total, held, *sems):
+        place = Place()
+        s1, r1, s2, r2, s3, r3, sg, rg = sems
+        me = place.f * 2 + place.c
+        barrier = pltpu.get_barrier_semaphore()
+
+        def plane(shift):
+            other = (me + shift) % 8
+            return (other // 2, other % 2, place.t)
+
+        for shift in range(1, 8):
+            pl.semaphore_signal(barrier, inc=1, device_id=plane(shift), device_id_type=MESH_ID)
+
+        @pl.when(place.outer)
+        def _():
+            pl.semaphore_signal(barrier, inc=1, device_id=place.chip_z(place.inner_mate), device_id_type=MESH_ID)
+            pl.semaphore_wait(barrier, 8)
+
+        @pl.when(jnp.logical_not(place.outer))
+        def _():
+            pl.semaphore_signal(barrier, inc=1, device_id=place.chip_z(place.outer_mate), device_id_type=MESH_ID)
+            pl.semaphore_signal(barrier, inc=1, device_id=place.chip_z(3 - place.t), device_id_type=MESH_ID)
+            pl.semaphore_wait(barrier, 9)
+
+        def cut(ref, i):
+            if isinstance(i, int):
+                return ref.at[pl.ds(i * step_rows, step_rows)]
+            return ref.at[pl.ds(pl.multiple_of(i * step_rows, step_rows), step_rows)]
+
+        def from_end(i, device):
+            return remote(cut(t_ref, i), cut(early, i), s1.at[i], r1.at[i], device)
+
+        def across(i):
+            return remote(cut(mid, i), cut(low, i), s2.at[i], r2.at[i], place.chip_z(3 - place.t))
+
+        def back(i, device):
+            return remote(cut(total, i), cut(total, i), s3.at[i], r3.at[i], device)
+
+        held[pl.ds(me, 1)] = dg_ref[...][None]
+        for shift in range(1, 8):
+            remote(dg_ref, held.at[me], sg.at[shift], rg.at[shift], plane(shift)).start()
+
+        @pl.when(place.outer)
+        def _():
+            for i in range(chunks):
+                from_end(i, place.chip_z(place.inner_mate)).start()
+
+        def pair_up(i):
+            @pl.when(jnp.logical_not(place.outer))
+            def _():
+                from_end(i, place.chip_z(place.outer_mate)).wait_recv()
+                pair = cut(t_ref, i)[...].astype(jnp.float32) + cut(early, i)[...].astype(jnp.float32)
+                cut(mid, i)[...] = pair.astype(mid.dtype)
+                across(i).start()
+
+        def join(i):
+            @pl.when(jnp.logical_not(place.outer))
+            def _():
+                across(i).wait_recv()
+                whole = cut(mid, i)[...].astype(jnp.float32) + cut(low, i)[...].astype(jnp.float32)
+                cut(total, i)[...] = whole.astype(total.dtype)
+                back(i, place.chip_z(place.outer_mate)).start()
+
+        norm_size = jnp.sqrt(n_ref[0:1, 0:1])
+        inverse = 1.0 / (norm_size + ortho_eps)
+        scale = inverse * inverse
+
+        for k in range(parts):
+            sl = pl.ds(k * tile, tile)
+            value = g_ref[sl] * scale
+            p_ref[sl] = value
+            high, rest = halves(value)
+            ph[sl] = high
+            pl_[sl] = rest
+        x_ref[...] = d_ref[...].astype(jnp.float32) * inverse
+
+        def product(lh, ll, rh, rl, k):
+            sl, cols = pl.ds(k * tile, tile), pl.ds(k * tile, width - k * tile)
+
+            def dot(left, right):
+                return jnp.dot(left[sl], right[:, cols], preferred_element_type=jnp.float32)
+
+            return dot(lh, rh) + dot(ll, rh) + dot(lh, rl)
+
+        def spread_out(value, high_ref, low_ref, k):
+            sl, cols = pl.ds(k * tile, tile), pl.ds(k * tile, width - k * tile)
+            high, rest = halves(value)
+            high_ref[sl, cols] = high
+            low_ref[sl, cols] = rest
+            for j in range(k + 1, parts):
+                at = (j - k) * tile
+                high_ref[pl.ds(j * tile, tile), sl] = high[:, at:at + tile].T
+                low_ref[pl.ds(j * tile, tile), sl] = rest[:, at:at + tile].T
+
+        def squares():
+            for k in range(parts):
+                sl, cols = pl.ds(k * tile, tile), pl.ds(k * tile, width - k * tile)
+                value = product(ph, pl_, ph, pl_, k)
+                spread_out(value, hh, hl, k)
+                mix = (ns_second * p_ref[sl, cols] + ns_third * value).astype(mx.dtype)
+                mx[sl, cols] = mix
+                for j in range(k + 1, parts):
+                    at = (j - k) * tile
+                    mx[pl.ds(j * tile, tile), sl] = mix[:, at:at + tile].T
+
+        def rotate_rows():
+            for at, size in ((0, 336), (336, 320)):
+                sl = pl.ds(at, size)
+                old = x_ref[sl]
+                x_ref[sl] = ns_first * old + jnp.dot(old.astype(jnp.bfloat16), mx[...], preferred_element_type=jnp.float32)
+
+        def body(sweep, carry):
+            pair_up(2 * sweep)
+            squares()
+            pair_up(2 * sweep + 1)
+
+            @pl.when(sweep >= 1)
+            def _():
+                join(2 * sweep - 2)
+            rotate_rows()
+            for k in range(parts):
+                sl, cols = pl.ds(k * tile, tile), pl.ds(k * tile, width - k * tile)
+                cube = product(ph, pl_, hh, hl, k)
+                square = hh[sl, cols].astype(jnp.float32) + hl[sl, cols].astype(jnp.float32)
+                spread_out(bc * square + cc * cube, uh, ul, k)
+                p_ref[sl, cols] = aa * p_ref[sl, cols] + ab * square + bbac * cube
+
+            @pl.when(sweep >= 1)
+            def _():
+                join(2 * sweep - 1)
+            for k in range(parts):
+                sl, cols = pl.ds(k * tile, tile), pl.ds(k * tile, width - k * tile)
+                value = p_ref[sl, cols] + product(hh, hl, uh, ul, k)
+                p_ref[sl, cols] = value
+                spread_out(value, ph, pl_, k)
+            return carry
+
+        lax.fori_loop(0, ITERS - 1, body, 0)
+        join(chunks - 2)
+        join(chunks - 1)
+        squares()
+        rotate_rows()
+        spread = jnp.where(place.f == 0, 0.2 * math.sqrt(3 * D), jnp.where(place.f == 1, 0.2 * math.sqrt(D), jnp.where(
+            place.f == 2, 0.2 * math.sqrt(2 * FF), 0.2 * math.sqrt(FF)))).astype(jnp.float32)
+        u_ref[...] = -muon_rate * (spread * x_ref[...] + decay_rate * w_ref[...].astype(jnp.float32))
+
+        for shift in range(1, 8):
+            remote(dg_ref, held.at[me], sg.at[shift], rg.at[shift], plane(shift)).wait()
+        grads = held[0]
+        for k in range(1, 8):
+            grads = grads + held[k]
+        gg_ref[...] = grads
+        first = adam_beta * af_ref[...] + (1.0 - adam_beta) * grads
+        second = adam_beta * as_ref[...] + (1.0 - adam_beta) * grads * grads
+        afn_ref[...] = first
+        asn_ref[...] = second
+        gu_ref[...] = -adam_rate * (
+            first / correction / (jnp.sqrt(second / correction) + adam_eps) + decay_rate * gain_ref[...]
+        )
+
+        @pl.when(place.outer)
+        def _():
+            for i in range(chunks):
+                back(i, place.chip_z(place.inner_mate)).wait_recv()
+                from_end(i, place.chip_z(place.inner_mate)).wait_send()
+        lo_ref[...] = (r_ref[...] + total[...].astype(jnp.float32)).astype(lo_ref.dtype)
+
+        @pl.when(jnp.logical_not(place.outer))
+        def _():
+            for i in range(chunks):
+                across(i).wait_send()
+                back(i, place.chip_z(place.outer_mate)).wait_send()
+
+    f32, low16 = jnp.float32, jnp.bfloat16
+    small = jax.ShapeDtypeStruct(dgains.shape, f32)
+    outs = (jax.ShapeDtypeStruct((rows, width), f32), jax.ShapeDtypeStruct((tokens, width), low16), small, small, small, small)
+    full = pltpu.VMEM((width, width), low16)
+    line = pltpu.VMEM((tokens, width), low16)
+    scratch = [pltpu.VMEM((width, width), f32)] + [full] * 7 + [pltpu.VMEM((rows, width), f32)] + [line] * 4
+    scratch += [pltpu.VMEM((8,) + dgains.shape, f32)] + [dma(chunks)] * 6 + [dma(8)] * 2
+    ins = (gram, norm, direction_low, own_block, branch_term, resid, dgains, norm_gains, adam_first, adam_second)
+    return comm_call(kernel, outs, ins, [VMEM_SPEC] * len(ins), (VMEM_SPEC,) * len(outs), scratch, ident)
 
 
 def per_device_block(tokens, out_grad, weight_stack, muon_state, norm_gains, adam_first, adam_second, segment_ids,
@@ -976,8 +1188,11 @@
         axis=1,
     ).astype(low)
     early_terms = jnp.concatenate([grad_term(dprojected, act_in), grad_term(attn_in, dbranch_one)], axis=0)
-    (grad_early,) = scatter_grads(early_terms, counts, (0, 1), local_rows, 5)
     dnormed_one_term = jnp.dot(dprojected, w_qkv, preferred_element_type=jnp.float32).astype(low)
+    grad_early, dnormed_one = scatter_grads(early_terms, counts, (0, 1), local_rows, 5, dnormed_one_term)
+    _, norm_one_pull = jax.vjp(layer_norm, inputs, norm_gains[0])
+    dinput_norm, dgain_one = norm_one_pull(dnormed_one.astype(jnp.float32))
+    tokens_grad = (dresid + dinput_norm).astype(low).reshape(tokens.shape)
 
     owner_index = lax.axis_index("fsdp")
     grad_block = jnp.where(owner_index >= 2, grad_late, grad_early)
@@ -987,52 +1202,12 @@
     direction_low = direction.astype(low)
     square = jnp.sum(direction * direction).reshape(1, 1)
     gram, norm_total = gram_sum(direction_low, jnp.broadcast_to(square, (8, 128)), 6)
-    norm_size = jnp.sqrt(norm_total[0, 0])
-    direction_scale = jnp.log(norm_size).reshape(1)
-    inverse = 1.0 / (norm_size + ortho_eps)
-    branch_two_term, dnormed_one_term, gram = lax.optimization_barrier((branch_two_term, dnormed_one_term, gram))
-    branch_two = lax.psum(branch_two_term, "tensor").astype(jnp.float32)
-    dnormed_one = lax.psum(dnormed_one_term, "tensor").astype(jnp.float32)
-
-    power = gram * (inverse * inverse)
-    ortho = direction_low.astype(jnp.float32) * inverse
-    high = lax.Precision.HIGH
-
-    def times(left, right):
-        return jnp.dot(left, right, precision=high, preferred_element_type=jnp.float32)
-
-    for sweep_index in range(ITERS):
-        square_power = times(power, power)
-        mix = ns_second * power + ns_third * square_power
-        ortho = ns_first * ortho + jnp.dot(ortho.astype(low), mix.astype(low), preferred_element_type=jnp.float32)
-        if sweep_index < ITERS - 1:
-            cube = times(power, square_power)
-            tail = (2.0 * ns_second * ns_third) * square_power + (ns_third * ns_third) * cube
-            power = (
-                (ns_first * ns_first) * power
-                + (2.0 * ns_first * ns_second) * square_power
-                + (ns_second * ns_second + 2.0 * ns_first * ns_third) * cube
-                + times(square_power, tail)
-            )
-
-    layer_out = (resid + branch_two).astype(low).reshape(tokens.shape)
-    _, norm_one_pull = jax.vjp(layer_norm, inputs, norm_gains[0])
-    dinput_norm, dgain_one = norm_one_pull(dnormed_one)
-    tokens_grad = (dresid + dinput_norm).astype(low).reshape(tokens.shape)
-    gain_grads = plane_sum(jnp.concatenate([jnp.stack([dgain_one, dgain_two])] * 4, axis=0), 7)[:2]
-    spreads = jnp.array(
-        [0.2 * math.sqrt(3 * D), 0.2 * math.sqrt(D), 0.2 * math.sqrt(2 * FF), 0.2 * math.sqrt(FF)],
-        jnp.float32,
-    )
-    spread = jnp.sum(jnp.where(jnp.arange(4) == owner_index, spreads, 0.0))
-    weight_update = -muon_rate * (spread * ortho + decay_rate * own_block.astype(jnp.float32))
-    adam_first_next = adam_beta * adam_first + (1.0 - adam_beta) * gain_grads
-    adam_second_next = adam_beta * adam_second + (1.0 - adam_beta) * gain_grads * gain_grads
-    correction = 1.0 - adam_beta**STEP
-    gain_update = -adam_rate * (
-        adam_first_next / correction / (jnp.sqrt(adam_second_next / correction) + adam_eps)
-        + decay_rate * norm_gains
-    )
+    direction_scale = jnp.log(jnp.sqrt(norm_total[0, 0])).reshape(1)
+    weight_update, layer_out, gain_grads, adam_first_next, adam_second_next, gain_update = iterate(
+        gram, norm_total, direction_low, own_block, branch_two_term, resid, jnp.stack([dgain_one, dgain_two]),
+        norm_gains, adam_first, adam_second, 7,
+    )
+    layer_out = layer_out.reshape(tokens.shape)
     block_shape = (1, 1, local_rows, model_width)
     return (
         layer_out,

time: 682 us -> 498 us (0.73)
  matrix products: 221 us -> 81.6 us
  Pallas kernels: 366 us -> 322 us
  between operations: 17.8 us -> 3.62 us
  local copies, waits for them, and re-layouts: 22.2 us -> 33.7 us
    dot_general x18 -> x0, matrix products: 138 us -> none  [the longest x13 117 us: times(): jnp.dot(left, right, precision=high, preferred_element_type=jnp.float32)]
    pallas_call x8, Pallas kernels: 366 us -> 322 us  [comm_call(): pl.pallas_call(kernel, out_shape=outs, in_specs=in_specs, out_specs=out_s...]
    unnamed x96, local copies, waits for them, and re-layouts: 3.84 us -> 14.9 us
  transfers between devices with their start and end apart: 1 -> 0, of which waited for: 0 -> 0; matrix products, arithmetic and copies ran while one was open for 21% -> 0% of each run, Pallas kernels for 0% -> 0%
where the time goes in v2:
time: 498 us; the launch traced here: 489 us
  Pallas kernels  322 us (65%)
  matrix products  81.6 us (16%)
  other arithmetic  48.4 us (10%)
  local copies, waits for them, and re-layouts  33.7 us (7%)
    pallas_call x8, Pallas kernels, comm_call(): pl.pallas_call(kernel, out_shape=outs, in_specs=in_specs, out_specs=out_s...  322 us
    dot_general x1, matrix products, per_device_block(): jnp.einsum('hlm,lhd->mhd', dscores, queries, preferred_element_type=jnp.f...  23.9 us
    dot_general x1, matrix products, per_device_block(): jnp.einsum('hlm,mhd->lhd', dscores, keys_all, preferred_element_type=jnp....  23 us
    unnamed x96, local copies, waits for them, and re-layouts  14.9 us

profile of v2, /device:TPU:0, one launch (start us, length us, event | category | flops | bytes accessed | tf_op | source)
XLA Modules:
  0.0 489.0 jit_solution(2688334350130295193)
XLA Ops:
  2.1 1.4 convert_reduce_fusion
  3.5 1.6 fusion.47
  8.2 25.9 %shard_map.168 = bf16[1024,1024]{1,0:T(8,128)(2,1)} custom-call(bf16[656,1024]{1,0:T(8,128)(2,1)} %bitcast.145), custom_call_target="tpu_custom_call" | custom-call | tf_op jit(solution)/shard_map/pallas_call | solution.py:633
  38.3 1.4 slice_bitcast_fusion
  39.9 1.3 fusion.87
  44.3 3.8 shard_map.169
  50.3 1.6 fusion.2
  51.9 2.4 exponential_reduce_fusion
  55.2 2.3 fusion.113
  57.6 1.4 convolution_convert_fusion.5.term_ref
  59.0 56.9 %shard_map.170 = (bf16[512,1024]{1,0:T(8,128)(2,1)}, bf16[1968,1024]{1,0:T(8,128)(2,1)}) custom-call(bf16[512,1024]{1,0:T(8,128)(2,1)} %convolution_convert_fusion.5.term_ref, bf16[656,1024]{1,0:T(8,128)(2,1)} %bitcast.146), custom_call_target="tpu_custom_call" | custom-call | tf_op jit(solution)/shard_map/pallas_call | solution.py:633
  115.9 1.7 fusion.116
  117.6 1.7 fusion.28
  120.5 1.8 fusion.40
  122.3 3.8 add_convert_fusion.1
  126.9 2.8 fusion.52.refs_1_
  129.6 2.0 convolution_convert_fusion.4.t_ref
  132.5 1.7 convolution_convert_fusion
  134.3 2.3 pad_maximum_fusion.refs_0_
  136.6 55.9 %shard_map.171 = (f32[656,1024]{1,0:T(8,128)}, bf16[512,1024]{1,0:T(8,128)(2,1)}) custom-call(bf16[1968,1024]{1,0:T(8,128)(2,1)} %pad_maximum_fusion.refs_0_, bf16[512,1024]{1,0:T(8,128)(2,1)} %fusion.52.refs_1_), custom_call_target="tpu_custom_call" | custom-call | tf_op jit(solution)/shard_map/pallas_call | solution.py:633
  192.6 3.0 fusion.45
  195.6 2.3 fusion.117
  198.3 1.2 copy-done.8
  200.0 1.2 convolution_convert_fusion.6
  201.3 3.2 fusion.111
  204.5 2.5 copy.39
  207.1 5.7 %fusion.125 = f32[4,512,1024]{2,1,0:T(8,128)} fusion(bf16[512,4,64]{0,2,1:T(8,128)(2,1)} %bitcast.166, bf16[1024,4,64]{0,2,1:T(8,128)(2,1)} %bitcast.154), kind=kOutput, calls=%fused_computation.185 | convolution fusion | flops 268435456 | bytes 9175040 | tf_op jit(solution)/shard_map/lhd,mhd->hlm/dot_general | solution.py:1172
  212.8 23.9 %fusion.7 = f32[4,64,1024]{2,1,0:T(8,128)} fusion(bf16[512,4,64]{0,2,1:T(8,128)(2,1)S(1)} %copy-done.21, f32[4,512,1024]{2,1,0:T(8,128)} %fusion.125, f32[4,512,1024]{2,1,0:T(8,128)} %copy-done.1, f32[4,512]{1,0:T(4,128)} %copy-done.34, pred[512,1024]{1,0:T(8,128)(4,1)} %broadcast_compare_fusion), kind=kOutput, calls=%fused_computation.9 | convolution fusion | flops 291507200 | bytes 18620416 | tf_op jit(solution)/shard_map/hlm,lhd->mhd/dot_general | solution.py:1176
  236.6 2.5 copy.38
  239.2 2.1 fusion.76.x_ref
  241.2 3.8 shard_map.172
  245.0 1.5 fusion.71
  248.4 2.0 copy.41
  250.4 23.0 %broadcast_multiply_fusion.1 = (f32[512,4,64]{0,2,1:T(8,128)}, f32[512,4,64]{0,2,1:T(8,128)}, f32[512,4,64]{0,2,1:T(8,128)}) fusion(f32[512,64]{0,1:T(8,128)S(1)} %copy-done.23, f32[512,4,64]{0,2,1:T(8,128)} %bitcast.164, bf16[1024,4,64]{0,2,1:T(8,128)(2,1)} %bitcast.152, f32[4,512,1024]{2,1,0:T(8,128)} %fusion.125, f32[4,512,1024]{2,1,0:T(8,128)} %copy-done.1, ...), kind=kOutput, calls=%fused_computation.142 | convolution fusion | flops 291769344 | bytes 20062208 | tf_op jit(solution)/shard_map/hlm,mhd->lhd/dot_general | solution.py:1175
  278.4 2.0 copy.42
  280.4 1.4 add_convert_fusion.2
  281.9 3.5 convolution_convert_fusion.3.refs_1_
  286.6 1.5 pad_maximum_fusion.1.refs_0_
  288.1 46.7 %shard_map.173 = (f32[656,1024]{1,0:T(8,128)}, bf16[512,1024]{1,0:T(8,128)(2,1)}) custom-call(bf16[1024,1024]{1,0:T(8,128)(2,1)} %pad_maximum_fusion.1.refs_0_, bf16[512,1024]{1,0:T(8,128)(2,1)} %convolution_convert_fusion.3.refs_1_), custom_call_target="tpu_custom_call" | custom-call | tf_op jit(solution)/shard_map/pallas_call | solution.py:633
  334.7 5.4 %fusion.42 = (f32[1,1,656,1024]{3,2,1,0:T(8,128)}, f32[656,1024]{1,0:T(8,128)S(1)}) fusion(f32[1,1,656,1024]{3,2,1,0:T(8,128)} %param.12, f32[656,1024]{1,0:T(8,128)} %get-tuple-element.26, f32[656,1024]{1,0:T(8,128)} %get-tuple-element.28, pred[]{:T(512)S(6)} %ge.3), kind=kLoop, calls=%fused_computation.47 | loop fusion | flops 2686976 | bytes 13434881 | tf_op jit(solution)/shard_map/reshape | solution.py:1216
  340.9 1.2 fusion.55
  342.2 1.9 fusion.85
  344.7 2.4 multiply_reduce_fusion.1
  347.1 1.2 broadcast_in_dim.26.q_ref
  348.4 47.7 %shard_map.174 = (f32[1024,1024]{1,0:T(8,128)}, f32[8,128]{1,0:T(8,128)}) custom-call(bf16[656,1024]{1,0:T(8,128)(2,1)} %get-tuple-element.51.x_ref.d_ref, f32[8,128]{1,0:T(8,128)} %broadcast_in_dim.26.q_ref), custom_call_target="tpu_custom_call" | custom-call | tf_op jit(solution)/shard_map/pallas_call | solution.py:633
  397.9 81.1 %shard_map.175 = (f32[656,1024]{1,0:T(8,128)}, bf16[512,1024]{1,0:T(8,128)(2,1)}, f32[2,1024]{1,0:T(2,128)}, f32[2,1024]{1,0:T(2,128)}, f32[2,1024]{1,0:T(2,128)}, /*index=5*/f32[2,1024]{1,0:T(2,128)}) custom-call(f32[1024,1024]{1,0:T(8,128)} %get-tuple-element.29.g_ref, f32[8,128]{1,0:T(8,128)} %get-tuple-element.30.n_ref, ...), custom_call_target="tpu_custom_call" | custom-call | tf_op jit(solution)/shard_map/pallas_call | solution.py:633
  479.0 2.3 copy.51
  481.3 3.7 copy.52
  (145 shorter events, 31.4 us)
Async XLA Ops:
  0.6 4.5 copy-start.40
  0.7 5.2 %copy-start.27 = (f32[2,1024]{1,0:T(2,128)S(1)}, f32[2,1024]{1,0:T(2,128)}, u32[]{:S(2)}) copy-start(f32[2,1024]{1,0:T(2,128)} %gain_ref.1) | copy-start | bytes 24580
  5.2 29.0 %copy-start.30 = (f32[512]{0:T(512)}, f32[512]{0:T(512)S(1)}, u32[]{:S(2)}) copy-start(f32[512]{0:T(512)S(1)} %fusion.47) | copy-start | bytes 6148
  5.2 29.0 %copy-start.28 = (f32[512]{0:T(512)}, f32[512]{0:T(512)S(1)}, u32[]{:S(2)}) copy-start(f32[512]{0:T(512)S(1)} %fusion.95) | copy-start | bytes 6148
  8.2 34.1 %copy-start.10 = (f32[512,256]{1,0:T(8,128)}, f32[512,256]{1,0:T(8,128)S(1)}, u32[]{:S(2)}) copy-start(f32[512,256]{1,0:T(8,128)S(1)} %copy.33) | copy-start | bytes 1572868
  34.1 1.2 copy-start
  34.1 1.7 slice-start.2
  37.0 1.1 copy-start.16
  38.3 1.6 copy-start.22
  41.1 8.6 %copy-start.20 = (bf16[512,4,64]{0,2,1:T(8,128)(2,1)}, bf16[512,4,64]{0,2,1:T(8,128)(2,1)S(1)}, u32[]{:S(2)}) copy-start(bf16[512,4,64]{0,2,1:T(8,128)(2,1)S(1)} %get-tuple-element.71) | copy-start | bytes 786436
  49.2 1.0 copy-start.11
  49.5 2.4 copy-start.17
  49.8 4.6 copy-start.18
  51.9 3.3 copy-start.1
  55.2 2.3 copy-start.34
  55.2 2.4 copy-start.7
  115.9 1.7 copy-start.2
  117.6 2.9 copy-start.42
  120.5 72.0 %copy-start.32 = (f32[512]{0:T(512)}, f32[512]{0:T(512)S(1)}, u32[]{:S(2)}) copy-start(f32[512]{0:T(512)S(1)} %fusion.96) | copy-start | bytes 6148
  120.5 1.8 copy-start.13
  192.5 3.1 copy-start.3
  192.5 5.4 %copy-start.14 = (bf16[512,1,1024]{2,0,1:T(8,128)(2,1)S(1)}, bf16[512,1,1024]{2,0,1:T(8,128)(2,1)}, u32[]{:S(2)}) copy-start(bf16[512,1,1024]{2,0,1:T(8,128)(2,1)} %param.10) | copy-start | bytes 3145732
  192.6 8.7 %slice-start = ((s8[8388608]{0:T(1024)(128)(4,1)}), s8[4194304]{0:T(1024)(128)(4,1)S(1)}, s32[]{:S(2)}) async-start(s8[8388608]{0:T(1024)(128)(4,1)} %bitcast.143), calls=%async_computation | async-start | bytes 8388608
  195.6 5.7 %slice-start.1 = ((s8[8388608]{0:T(1024)(128)(4,1)}), s8[4194304]{0:T(1024)(128)(4,1)S(1)}, s32[]{:S(2)}) async-start(s8[8388608]{0:T(1024)(128)(4,1)} %bitcast.143), calls=%async_computation.1 | async-start | bytes 8388608
  198.0 1.6 copy-start.8
  198.0 1.6 copy-start.41
  199.5 1.8 copy-start.12
  199.5 1.8 copy-start.35
  200.0 4.5 copy-start.24
  207.1 5.7 %copy-start.21 = (bf16[512,4,64]{0,2,1:T(8,128)(2,1)S(1)}, bf16[512,4,64]{0,2,1:T(8,128)(2,1)}, u32[]{:S(2)}) copy-start(bf16[512,4,64]{0,2,1:T(8,128)(2,1)} %copy-done.20) | copy-start | bytes 786436
  246.5 1.1 copy-start.9
  246.5 3.9 copy-start.23
  277.6 4.3 copy-start.25
  281.9 3.5 copy-start.26
  281.9 3.5 copy-start.29
  285.4 1.2 copy-start.19
  334.7 5.4 %copy-start.6 = (bf16[512,1024]{1,0:T(8,128)(2,1)S(1)}, bf16[512,1024]{1,0:T(8,128)(2,1)}, u32[]{:S(2)}) copy-start(bf16[512,1024]{1,0:T(8,128)(2,1)} %get-tuple-element.31) | copy-start | bytes 3145732
  340.2 4.5 copy-start.5
  340.2 0.7 copy-start.31
  340.2 2.0 copy-start.15
  342.2 1.9 copy-start.33
  342.2 2.5 copy-start.4
  481.3 3.7 copy-start.39
  481.3 4.3 copy-start.38
  481.3 4.9 copy-start.37
  481.3 5.5 %copy-start.36 = (f32[2,1024]{1,0:T(2,128)S(1)}, f32[2,1024]{1,0:T(2,128)}, u32[]{:S(2)}) copy-start(f32[2,1024]{1,0:T(2,128)} %get-tuple-element.102) | copy-start | bytes 24580
